TPU v7x, 8 devices: a whole 2x2x1 slice. The times are simulated.
8 devices in a mesh: dp: 1 (over z), sp: 8 (over y, x, core).
Axes of the slice: x: 2, y: 2, z: 1, core: 2. Of those that a mesh axis runs over, the one named last changes fastest.
Arguments:
- hidden: bfloat16 [16, 128, 2560], P('dp', 'sp')
- attn_norm: bfloat16 [2560], replicated
- w_q: bfloat16 [2560, 32, 128], replicated
- w_k: bfloat16 [2560, 8, 128], replicated
- w_v: bfloat16 [2560, 8, 128], replicated
- w_o: bfloat16 [32, 128, 2560], replicated
- mlp_norm: bfloat16 [2560], replicated
- w_gate: bfloat16 [2560, 9728], replicated
- w_up: bfloat16 [2560, 9728], replicated
- w_down: bfloat16 [9728, 2560], replicated
- mamba_norm: bfloat16 [2560], replicated
- w_in_x: bfloat16 [2560, 5120], replicated
- w_in_z: bfloat16 [2560, 5120], replicated
- conv_w: bfloat16 [4, 5120], replicated
- conv_b: bfloat16 [5120], replicated
- w_xproj: bfloat16 [5120, 192], replicated
- dt_norm: float32 [160], replicated
- b_norm: float32 [16], replicated
- c_norm: float32 [16], replicated
- w_dt: bfloat16 [160, 5120], replicated
- dt_bias: float32 [5120], replicated
- a_log: float32 [5120, 16], replicated
- d_skip: float32 [5120], replicated
- w_out: bfloat16 [5120, 2560], replicated
Outputs:
- output: bfloat16 [16, 128, 2560], P('dp', 'sp')
All inputs are finite; a program needn't handle non-finite values.
Results may differ from a plain program's by a relative error of at most 0.02.
Values are sent between devices in bfloat16 or wider.
A program may use at most 1.25 GiB of HBM per device.

v0:
```python
import functools
import jax
import jax.numpy as jnp
from jax import lax
from jax.sharding import PartitionSpec as P

EPS = 1e-6
CONV = 4


def rms_scale(values, gain_vec):
    values_f = values.astype(jnp.float32)
    inv_rms = lax.rsqrt(jnp.mean(values_f * values_f, axis=-1, keepdims=True) + EPS)
    return values_f * inv_rms * gain_vec.astype(jnp.float32)


def attention_layer(hidden, attn_norm, w_q, w_k, w_v, w_o):
    n_batch, tok_local, model_dim = hidden.shape
    n_heads, head_dim = w_q.shape[1], w_q.shape[2]
    kv_heads = w_k.shape[1]
    groups = n_heads // kv_heads
    normed = rms_scale(hidden, attn_norm).astype(jnp.bfloat16).reshape(n_batch * tok_local, model_dim)
    queries = jnp.dot(normed, w_q.reshape(model_dim, n_heads * head_dim), preferred_element_type=jnp.float32)
    queries = queries.astype(jnp.bfloat16).reshape(n_batch, tok_local, kv_heads, groups, head_dim)
    key_proj = jnp.dot(normed, w_k.reshape(model_dim, kv_heads * head_dim), preferred_element_type=jnp.float32)
    key_proj = key_proj.astype(jnp.bfloat16).reshape(n_batch, tok_local, kv_heads, head_dim)
    val_proj = jnp.dot(normed, w_v.reshape(model_dim, kv_heads * head_dim), preferred_element_type=jnp.float32)
    val_proj = val_proj.astype(jnp.bfloat16).reshape(n_batch, tok_local, kv_heads, head_dim)
    queries = lax.all_to_all(queries, "sp", 2, 1, tiled=True)
    key_proj = lax.all_to_all(key_proj, "sp", 2, 1, tiled=True)
    val_proj = lax.all_to_all(val_proj, "sp", 2, 1, tiled=True)
    seq_len = key_proj.shape[1]
    causal = lax.broadcasted_iota(jnp.int32, (seq_len, 1), 0) >= lax.broadcasted_iota(jnp.int32, (1, seq_len), 1)
    scores = jnp.einsum("bqngd,bsnd->bngqs", queries, key_proj, preferred_element_type=jnp.float32) * head_dim ** -0.5
    scores = jnp.where(causal, scores, -jnp.inf)
    attn_prob = jax.nn.softmax(scores, axis=-1).astype(jnp.bfloat16)
    attn_out = jnp.einsum("bngqs,bsnd->bqngd", attn_prob, val_proj, preferred_element_type=jnp.float32).astype(jnp.bfloat16)
    attn_out = lax.all_to_all(attn_out, "sp", 1, 2, tiled=True)
    proj_out = jnp.dot(attn_out.reshape(n_batch * tok_local, n_heads * head_dim), w_o.reshape(n_heads * head_dim, model_dim), preferred_element_type=jnp.float32)
    return (hidden.astype(jnp.float32) + proj_out.reshape(n_batch, tok_local, model_dim)).astype(jnp.bfloat16)


def mlp_layer(hidden, mlp_norm, w_gate, w_up, w_down):
    model_dim = hidden.shape[-1]
    normed = rms_scale(hidden, mlp_norm).astype(jnp.bfloat16).reshape(-1, model_dim)
    gate_pre = jnp.dot(normed, w_gate, preferred_element_type=jnp.float32)
    up_proj = jnp.dot(normed, w_up, preferred_element_type=jnp.float32)
    act_val = (jax.nn.silu(gate_pre) * up_proj).astype(jnp.bfloat16)
    down_out = jnp.dot(act_val, w_down, preferred_element_type=jnp.float32)
    return (hidden.astype(jnp.float32) + down_out.reshape(hidden.shape)).astype(jnp.bfloat16)


def mamba_mixer(hidden, mamba_norm, w_in_x, w_in_z, conv_w, conv_b, w_xproj, dt_norm, b_norm, c_norm, w_dt, dt_bias, a_log, d_skip, w_out, n_shards):
    n_batch, tok_local, model_dim = hidden.shape
    n_inner, n_state = a_log.shape
    dt_rank = w_dt.shape[0]
    normed = rms_scale(hidden, mamba_norm).astype(jnp.bfloat16)
    x_inner = jnp.einsum("btd,de->tbe", normed, w_in_x, preferred_element_type=jnp.float32).astype(jnp.bfloat16)
    z_gate = jnp.einsum("btd,de->tbe", normed, w_in_z, preferred_element_type=jnp.float32).astype(jnp.bfloat16)
    shard_idx = lax.axis_index("sp")
    halo_rows = lax.ppermute(x_inner[tok_local - (CONV - 1):], "sp", [(src_idx, src_idx + 1) for src_idx in range(n_shards - 1)])
    padded = jnp.concatenate([halo_rows, x_inner], axis=0)
    conv_acc = conv_b.astype(jnp.float32)
    for tap_idx in range(CONV):
        conv_acc = conv_acc + padded[tap_idx:tap_idx + tok_local].astype(jnp.float32) * conv_w[tap_idx].astype(jnp.float32)
    x_conv = jax.nn.silu(conv_acc).astype(jnp.bfloat16)
    x_dbl = jnp.einsum("tbe,er->tbr", x_conv, w_xproj, preferred_element_type=jnp.float32)
    dt_in = rms_scale(x_dbl[..., :dt_rank], dt_norm).astype(jnp.bfloat16)
    b_mat = rms_scale(x_dbl[..., dt_rank:dt_rank + n_state], b_norm)
    c_mat = rms_scale(x_dbl[..., dt_rank + n_state:], c_norm)
    step_size = jax.nn.softplus(jnp.einsum("tbr,re->tbe", dt_in, w_dt, preferred_element_type=jnp.float32) + dt_bias)
    a_mat = -jnp.exp(a_log)

    def local_step(ssm_state, inputs):
        step_t, x_t, b_t, c_t = inputs
        decay_t = jnp.exp(step_t[:, :, None] * a_mat)
        ssm_state = decay_t * ssm_state + (step_t * x_t.astype(jnp.float32))[:, :, None] * b_t[:, None, :]
        return ssm_state, jnp.sum(ssm_state * c_t[:, None, :], axis=-1)

    def carry_step(ssm_state, inputs):
        step_t, c_t = inputs
        ssm_state = jnp.exp(step_t[:, :, None] * a_mat) * ssm_state
        return ssm_state, jnp.sum(ssm_state * c_t[:, None, :], axis=-1)

    zero_state = jnp.zeros((n_batch, n_inner, n_state), jnp.float32)
    end_state, y_local = lax.scan(local_step, zero_state, (step_size, x_conv, b_mat, c_mat))
    step_total = jnp.sum(step_size, axis=0)
    all_states = lax.all_gather(end_state, "sp")
    all_totals = lax.all_gather(step_total, "sp")
    preceding = jnp.arange(n_shards) < shard_idx
    prec_mask = preceding[:, None, None]
    before_total = jnp.sum(jnp.where(prec_mask, all_totals, 0.0), axis=0)
    gap_sum = jnp.where(prec_mask, before_total[None] - jnp.cumsum(all_totals, axis=0), 0.0)
    carry_weight = jnp.where(preceding[:, None, None, None], jnp.exp(gap_sum[..., None] * a_mat), 0.0)
    start_state = jnp.sum(carry_weight * all_states, axis=0)
    y_carry = lax.scan(carry_step, start_state, (step_size, c_mat))[1]
    y_total = y_local + y_carry + d_skip * x_conv.astype(jnp.float32)
    gated_y = (y_total * jax.nn.silu(z_gate.astype(jnp.float32))).astype(jnp.bfloat16)
    mamba_out = jnp.einsum("tbe,ed->btd", gated_y, w_out, preferred_element_type=jnp.float32)
    return (hidden.astype(jnp.float32) + mamba_out).astype(jnp.bfloat16)


def layer_pair(hidden, attn_norm, w_q, w_k, w_v, w_o, mlp_norm, w_gate, w_up, w_down, mamba_norm, w_in_x, w_in_z, conv_w, conv_b, w_xproj, dt_norm, b_norm, c_norm, w_dt, dt_bias, a_log, d_skip, w_out, n_shards):
    after_attn = attention_layer(hidden, attn_norm, w_q, w_k, w_v, w_o)
    after_mlp = mlp_layer(after_attn, mlp_norm, w_gate, w_up, w_down)
    return mamba_mixer(after_mlp, mamba_norm, w_in_x, w_in_z, conv_w, conv_b, w_xproj, dt_norm, b_norm, c_norm, w_dt, dt_bias, a_log, d_skip, w_out, n_shards)


def solution(mesh):
    act_spec = P("dp", "sp", None)
    return jax.shard_map(
        functools.partial(layer_pair, n_shards=mesh.shape["sp"]),
        mesh=mesh,
        in_specs=(act_spec,) + (P(),) * 23,
        out_specs=act_spec,
        check_vma=False,
    )
```

profile of v0, /device:TPU:0, one launch (start us, length us, event | category | flops | bytes accessed | tf_op | source)
XLA Modules:
  0.0 969.4 jit_solution(14160698393888644596)
XLA Ops:
  32.4 15.9 %fusion.38 = bf16[256,4096]{1,0:T(8,128)(2,1)} fusion(bf16[256,2560]{1,0:T(8,128)(2,1)} %bitcast.216, bf16[320,8,32,128]{3,2,1,0:T(8,128)(2,1)} %bitcast.225), kind=kOutput, calls=%fused_computation.45 | convolution fusion | flops 5369757696 | bytes 24379392 | tf_op jit(solution)/shard_map/dot_general | solution.py:23
  62.1 24.8 %all-to-all-done.2 = bf16[16,16,8,4,128]{4,3,1,0,2:T(4,128)(2,1)} async-done(((bf16[16,16,8,4,128]{4,3,1,0,2:T(4,128)(2,1)}), bf16[16,16,8,4,128]{4,3,1,0,2:T(4,128)(2,1)}, u32[]{:S(2)}, u32[]{:S(2)}) %all-to-all-start.2) | async-done | bytes 2097184 | tf_op jit(solution)/shard_map/all_to_all | solution.py:29
  101.8 26.3 %all-to-all-done.3 = bf16[16,128,1,4,128]{4,3,0,2,1:T(4,128)(2,1)} async-done(((bf16[16,128,1,4,128]{4,3,0,2,1:T(4,128)(2,1)}), bf16[16,128,1,4,128]{4,3,0,2,1:T(4,128)(2,1)}, u32[]{:S(2)}, u32[]{:S(2)}) %all-to-all-start.3) | async-done | bytes 2097184 | tf_op jit(solution)/shard_map/all_to_all | solution.py:38
  138.8 10.8 %fusion.61 = (f32[16,16]{1,0:T(8,128)S(1)}, bf16[16,16,2560]{2,1,0:T(8,128)(2,1)S(1)}) fusion(bf16[16,16,4096]{2,1,0:T(8,128)(2,1)} %dot_general.49, bf16[4096,2560,1]{1,0,2:T(8,128)(2,1)} %bitcast.226, bf16[16,16,2560]{2,1,0:T(8,128)(2,1)} %param.28), kind=kOutput, calls=%fused_computation.71 | convolution fusion | flops 5372641280 | bytes 25691136 | tf_op jit(solution)/shard_map/dot_general | solution.py:39
  152.1 23.8 %fusion.112 = f32[256,9728]{1,0:T(8,128)} fusion(bf16[256,2560]{1,0:T(8,128)(2,1)S(1)} %bitcast.217, bf16[2560,9728]{1,0:T(8,128)(2,1)} %param.35), kind=kOutput, calls=%fused_computation.127 | convolution fusion | flops 12750684160 | bytes 61079552 | tf_op jit(solution)/shard_map/dot_general | solution.py:46
  176.0 24.9 %fusion.10.clone.4 = bf16[256,9728]{1,0:T(8,128)(2,1)} fusion(bf16[256,2560]{1,0:T(8,128)(2,1)} %bitcast.218, bf16[2560,9728]{1,0:T(8,128)(2,1)} %param.36, f32[256,9728]{1,0:T(8,128)} %fusion.112), kind=kOutput, calls=%fused_computation.23.clone.clone.clone.1 | convolution fusion | flops 12765626368 | bytes 66060288 | tf_op jit(solution)/shard_map/dot_general | solution.py:47
  200.9 21.8 %fusion.11 = f32[256,2560]{1,0:T(8,128)S(1)} fusion(bf16[9728,2560]{1,0:T(8,128)(2,1)} %param.37, bf16[256,9728]{1,0:T(8,128)(2,1)} %fusion.10.clone.4), kind=kOutput, calls=%fused_computation.24 | convolution fusion | flops 12750684160 | bytes 57409536 | tf_op jit(solution)/shard_map/dot_general | solution.py:49
  223.2 12.9 %fusion.28 = bf16[16,16,5120]{2,0,1:T(8,128)(2,1)S(1)} fusion(bf16[2560,5120]{1,0:T(8,128)(2,1)} %param.39, bf16[16,16,2560]{2,1,0:T(8,128)(2,1)S(1)} %get-tuple-element.203, f32[2560]{0:T(1024)S(1)} %convert_element_type.174, f32[16,16]{1,0:T(8,128)S(1)} %add_rsqrt_fusion.3), kind=kOutput, calls=%fused_computation.35 | convolution fusion | flops 6714818560 | bytes 30157824 | tf_op jit(solution)/shard_map/btd,de->tbe/dot_general | solution.py:58
  241.4 8.3 multiply_convert_fusion.1
  254.5 8.0 fusion.111
  266.0 224.4 %while.26 = (s32[]{:T(128)}, f32[16,5120,16]{1,2,0:T(8,128)}, f32[16,16,5120]{2,0,1:T(8,128)}, f32[16,16,5120]{2,1,0:T(8,128)}, f32[5120,16]{0,1:T(8,128)S(1)}, ...) while((s32[]{:T(128)}, f32[16,5120,16]{1,2,0:T(8,128)}, ...), condition=%wide.region_10.11_spmd.clone, body=%wide.region_8.10_spmd.clone.sunk | while | flops 9256963 | bytes 14588035 | solution.py:86
  272.3 6.3 dynamic_update_slice.11
  286.4 6.3 dynamic_update_slice.11
  300.6 6.3 dynamic_update_slice.11
  314.7 6.3 dynamic_update_slice.11
  328.8 6.3 dynamic_update_slice.11
  343.0 6.3 dynamic_update_slice.11
  357.1 6.3 dynamic_update_slice.11
  371.2 6.3 dynamic_update_slice.11
  496.1 193.4 %all-gather.7.cloned.1.call-done = f32[128,5120,16]{1,2,0:T(8,128)} async-done(((f32[16,5120,16]{1,2,0:T(8,128)}), f32[128,5120,16]{1,2,0:T(8,128)}) %all-gather.7.cloned.1.call-update) | async-done | bytes 41943056 | tf_op jit(solution)/shard_map/all_gather | solution.py:88
  689.5 17.6 %multiply_reduce_fusion.2 = f32[16,5120,16]{1,2,0:T(8,128)} fusion(f32[8,16,5120,16]{2,3,1,0:T(8,128)} %bitcast.202, f32[5120,16]{0,1:T(8,128)S(1)} %get-tuple-element.368, f32[8,16,5120]{2,1,0:T(8,128)} %fusion.31, pred[8]{0:T(512)(128)(4,1)S(1)} %iota_compare_fusion.1), kind=kLoop, calls=%fused_computation.11 | loop fusion | flops 40632320 | bytes 50135048 | tf_op jit(solution)/shard_map/reduce_sum | solution.py:95
  710.1 220.7 %while.25 = (s32[]{:T(128)}, f32[16,5120,16]{1,2,0:T(8,128)}, f32[16,16,5120]{2,0,1:T(8,128)}, f32[16,16,5120]{2,1,0:T(8,128)}, f32[5120,16]{0,1:T(8,128)S(1)}, ...) while((s32[]{:T(128)}, f32[16,5120,16]{1,2,0:T(8,128)}, f32[16,16,5120]{2,0,1:T(8,128)}, ...), condition=%wide.region_17.18_spmd, body=%wide.region_15.17_spmd.sunk | while | flops 5160962 | bytes 13438049 | solution.py:96
  731.4 6.3 dynamic_update_slice.10
  827.9 6.3 dynamic_update_slice.10
  841.7 6.3 dynamic_update_slice.10
  855.5 6.3 dynamic_update_slice.10
  869.3 6.3 dynamic_update_slice.10
  883.1 6.3 dynamic_update_slice.10
  896.9 6.3 dynamic_update_slice.10
  910.7 6.3 dynamic_update_slice.10
  924.5 6.3 dynamic_update_slice.10
  930.8 31.6 %fusion.48 = bf16[16,16,2560]{2,1,0:T(8,128)(2,1)} fusion(bf16[5120,2560]{1,0:T(8,128)(2,1)} %param.51, bf16[16,16,2560]{2,1,0:T(8,128)(2,1)} %copy-done.7, bf16[16,16,5120]{2,0,1:T(8,128)(2,1)} %copy-done.2, f32[16,16,5120]{2,0,1:T(8,128)} %get-tuple-element.80, f32[16,16,5120]{2,0,1:T(8,128)} %get-tuple-element.82, bf16[2560,5120]{1,0:T(8,128)(2,1)} %param.40, ...), kind=kOutput, calls=%fused_computation.64 | convolution fusion | flops 13442088960 | bytes 68189184 | tf_op jit(solution)/shard_map/tbe,ed->btd/dot_general | solution.py:99
  (287 shorter events, 426.6 us)
Async XLA Ops:
  6.5 243.2 %copy-start = (bf16[5120,192]{0,1:T(8,128)(2,1)S(1)}, bf16[5120,192]{0,1:T(8,128)(2,1)}, u32[]{:S(2)}) copy-start(bf16[5120,192]{0,1:T(8,128)(2,1)} %param.43) | copy-start | bytes 5898244
  10.7 4.5 copy-start.8
  16.2 13.9 %all-to-all-start.1 = ((bf16[16,16,8,128]{3,1,0,2:T(8,128)(2,1)}), bf16[16,16,8,128]{3,1,0,2:T(8,128)(2,1)S(1)}, u32[]{:S(2)}, u32[]{:S(2)}) async-start(bf16[16,16,8,128]{3,1,0,2:T(8,128)(2,1)} %copy.97), calls=%async_computation.1 | async-start | bytes 1048576 | tf_op jit(solution)/shard_map/all_to_all | solution.py:30
  30.1 26.7 %all-to-all-start = ((bf16[16,16,8,128]{3,1,0,2:T(8,128)(2,1)}), bf16[16,16,8,128]{3,1,0,2:T(8,128)(2,1)S(1)}, u32[]{:S(2)}, u32[]{:S(2)}) async-start(bf16[16,16,8,128]{3,1,0,2:T(8,128)(2,1)} %copy.95), calls=%async_computation | async-start | bytes 1048576 | tf_op jit(solution)/shard_map/all_to_all | solution.py:31
  56.8 30.1 %all-to-all-start.2 = ((bf16[16,16,8,4,128]{4,3,1,0,2:T(4,128)(2,1)}), bf16[16,16,8,4,128]{4,3,1,0,2:T(4,128)(2,1)}, u32[]{:S(2)}, u32[]{:S(2)}) async-start(bf16[16,16,8,4,128]{4,3,1,0,2:T(4,128)(2,1)} %copy.99), calls=%async_computation.2 | async-start | bytes 4194304 | tf_op jit(solution)/shard_map/all_to_all | solution.py:29
  61.3 27.8 %copy-start.6 = (bf16[16,8,16,1,128]{4,2,1,0,3:T(8,128)(2,1)S(1)}, bf16[16,8,16,1,128]{4,2,1,0,3:T(8,128)(2,1)}, u32[]{:S(2)}) copy-start(bf16[16,8,16,1,128]{4,2,1,0,3:T(8,128)(2,1)} %copy.98) | copy-start | bytes 1572868
  89.0 2.0 copy-start.10
  93.9 7.8 copy-start.14
  93.9 7.8 copy-start.15
  93.9 7.8 copy-start.11
  98.5 29.6 %all-to-all-start.3 = ((bf16[16,128,1,4,128]{4,3,0,2,1:T(4,128)(2,1)}), bf16[16,128,1,4,128]{4,3,0,2,1:T(4,128)(2,1)}, u32[]{:S(2)}, u32[]{:S(2)}) async-start(bf16[16,128,1,4,128]{4,3,0,2,1:T(4,128)(2,1)} %copy.103), calls=%async_computation.3 | async-start | bytes 4194304 | tf_op jit(solution)/shard_map/all_to_all | solution.py:38
  101.6 388.9 %all-gather.5.cloned.1.call-start = ((), (), s32[]{:S(2)}) async-start(), calls=%async_computation.4 | async-start | bytes 2949120 | tf_op jit(solution)/shard_map/all_gather | solution.py:89
  149.6 1.1 copy-start.3
  151.1 1.1 copy-start.9
  200.9 21.8 %copy-start.4 = (bf16[16,16,2560]{2,1,0:T(8,128)(2,1)S(1)}, bf16[16,16,2560]{2,1,0:T(8,128)(2,1)}, u32[]{:S(2)}) copy-start(bf16[16,16,2560]{2,1,0:T(8,128)(2,1)} %copy-done.3) | copy-start | bytes 3932164
  223.2 13.0 %copy-start.7 = (bf16[16,16,2560]{2,1,0:T(8,128)(2,1)}, bf16[16,16,2560]{2,1,0:T(8,128)(2,1)S(1)}, u32[]{:S(2)}) copy-start(bf16[16,16,2560]{2,1,0:T(8,128)(2,1)S(1)} %get-tuple-element.203) | copy-start | bytes 3932164
  223.2 16.4 %copy-start.12 = (bf16[4,5120]{1,0:T(4,128)(2,1)S(1)}, bf16[4,5120]{1,0:T(4,128)(2,1)}, u32[]{:S(2)}) copy-start(bf16[4,5120]{1,0:T(4,128)(2,1)} %param.41) | copy-start | bytes 122884
  223.2 16.4 %copy-start.13 = (bf16[5120]{0:T(1024)(128)(2,1)S(1)}, bf16[5120]{0:T(1024)(128)(2,1)}, u32[]{:S(2)}) copy-start(bf16[5120]{0:T(1024)(128)(2,1)} %param.42) | copy-start | bytes 30724
  236.2 1.5 copy-start.5
  238.2 2.8 collective-permute-start
  249.8 1.5 copy-start.2
  249.8 4.6 copy-start.16
  249.8 4.7 copy-start.19
  254.5 8.4 copy-start.17
  254.5 8.4 copy-start.18
  262.5 427.0 %all-gather.7.cloned.1.call-start = ((), (), s32[]{:S(2)}) async-start(), calls=%async_computation.5 | async-start | bytes 47185920 | tf_op jit(solution)/shard_map/all_gather | solution.py:88
  710.1 220.7 %copy-start.20 = (f32[5120]{0:T(1024)S(1)}, f32[5120]{0:T(1024)}, u32[]{:S(2)}) copy-start(f32[5120]{0:T(1024)} %param.50) | copy-start | bytes 61444
  930.8 31.6 %copy-start.1 = (bf16[5120,192]{0,1:T(8,128)(2,1)S(1)}, bf16[5120,192]{0,1:T(8,128)(2,1)}, u32[]{:S(2)}) copy-start(bf16[5120,192]{0,1:T(8,128)(2,1)} %param.43) | copy-start | bytes 5898244
Sparse Core Ops, SparseCore 0:
  262.6 31.4 all-gather.4
  490.6 198.8 all-gather.6
where the time goes:
time: 983 us; the launch traced here: 969 us
  local copies, waits for them, and re-layouts  289 us (29%)
  waiting for transfers between devices  250 us (25%)
  other arithmetic  237 us (24%)
  matrix products  163 us (17%)
  starting transfers between devices  14.6 us (1%)
  between operations  14.1 us (1%)
    dynamic_update_slice x64, local copies, waits for them, and re-layouts, mamba_mixer(): lax.scan(local_step, zero_state, (step_size, x_conv, b_mat, c_mat))  213 us
    all_gather x1, waiting for transfers between devices, mamba_mixer(): all_states = lax.all_gather(end_state, 'sp')  193 us
    reduce_sum x16, other arithmetic, carry_step(): return (ssm_state, jnp.sum(ssm_state * c_t[:, None, :], axis=-1))  97.8 us
    reduce_sum x16, other arithmetic, local_step(): return (ssm_state, jnp.sum(ssm_state * c_t[:, None, :], axis=-1))  83.4 us
    dot_general x1, matrix products, mamba_mixer(): jnp.einsum('tbe,ed->btd', gated_y, w_out, preferred_element_type=jnp.floa...  31.6 us
    all_to_all x1, waiting for transfers between devices, attention_layer(): attn_out = lax.all_to_all(attn_out, 'sp', 1, 2, tiled=True)  26.3 us
    dot_general x1, matrix products, mlp_layer(): up_proj = jnp.dot(normed, w_up, preferred_element_type=jnp.float32)  24.9 us
    all_to_all x1, waiting for transfers between devices, attention_layer(): queries = lax.all_to_all(queries, 'sp', 2, 1, tiled=True)  24.8 us
  transfers between devices with their start and end apart: 7, of which 5 were waited for; matrix products, arithmetic and copies ran while one was open for 27% of the time, Pallas kernels for 0%

commit v1 on v0

v1 whole, which is shorter than its diff:
```python
import functools
import math
import jax
import jax.numpy as jnp
from jax import lax
from jax.experimental import pallas as pl
from jax.experimental.pallas import tpu as pltpu
from jax.sharding import PartitionSpec as P

EPS = 1e-6
CONV = 4
SLOTS = 9
WN = 512
PITCH = 41
F32 = jnp.float32
BF16 = jnp.bfloat16
LOG2E = math.log2(math.e)


def rms_scale(values, gain_vec):
    values_f = values.astype(F32)
    inv_rms = lax.rsqrt(jnp.mean(values_f * values_f, axis=-1, keepdims=True) + EPS)
    return values_f * inv_rms * gain_vec.astype(F32)


def silu(v):
    half = 0.5 * v
    return half + half * jnp.tanh(half)


def block_kernel(q_hbm, k_hbm, v_hbm, x_hbm, wo, wg, wu, wd, wx, wz, wxp_hbm, wdt_hbm, wout,
                 norms, chan, gains, dskip, a2, out_ref,
                 ring, qo, kbuf, vbuf, h, a, act, xc, zg, delta, xs, bb, cb, wxp, wdt,
                 ring_sem, in_sem):
    rows, dim = h.shape
    seq = 128
    n_seq = rows // seq
    inner = wx.shape[1]
    ff = wg.shape[1]
    qdim = wo.shape[0]
    kv_heads = kbuf.shape[1] // 128
    groups = qdim // kbuf.shape[1]
    lanes = inner // 128
    n_state = a2.shape[0] // lanes
    dt_rank = wdt.shape[0]
    unit = ring.shape[1]

    def chunks(total):
        return [(s, min(unit, total - s)) for s in range(0, total, unit)]

    def cols(t):
        return pl.ds(pl.multiple_of(t * WN, WN), WN)

    segs = []
    base = 0

    def add_seg(n_tiles, parts):
        nonlocal base
        first = base
        base = first + n_tiles * len(parts)
        segs.append((first, base, parts))
        return first

    half_q = qdim // 2
    u_wo = add_seg(dim // WN, [(wo, 0, half_q), (wo, half_q, half_q)])
    u_gu = add_seg(ff // WN, [(wg, 0, dim), (wu, 0, dim)])
    u_dn = add_seg(dim // WN, [(wd, s, n) for s, n in chunks(ff)])
    u_wx = add_seg(inner // WN, [(wx, 0, dim)])
    u_wz = add_seg(inner // WN, [(wz, 0, dim)])
    u_out = add_seg(dim // WN, [(wout, s, n) for s, n in chunks(inner)])

    def copy(part, tile, slot):
        w, r0, nr = part
        return pltpu.make_async_copy(w.at[pl.ds(r0, nr), cols(tile)], ring.at[slot, pl.ds(0, nr)], ring_sem.at[slot])

    def start(u, lo, hi):
        for first, last, parts in segs:
            if hi < first or lo >= last:
                continue
            n = len(parts)
            for i, part in enumerate(parts):
                @pl.when((u >= first) & (u < last) & (lax.rem(u - first + n, n) == i))
                def _(part=part, first=first, n=n):
                    copy(part, lax.div(u - first, n), lax.rem(u, SLOTS)).start()

    def phase(first, n_tiles, body):
        parts = [s for s in segs if s[0] == first][0][2]
        n = len(parts)

        @pl.loop(0, n_tiles)
        def _(t):
            vals = []
            for i, part in enumerate(parts):
                slot = lax.rem(first + t * n + i, SLOTS)
                copy(part, 0, slot).wait()
                vals.append(ring.at[slot, pl.ds(0, part[2])])
            body(t, *vals)
            for i in range(n):
                start(first + t * n + i + SLOTS, first + SLOTS, first + SLOTS + n_tiles * n - 1)

    in_copies = [
        pltpu.make_async_copy(q_hbm, qo, in_sem.at[0]),
        pltpu.make_async_copy(k_hbm, kbuf, in_sem.at[1]),
        pltpu.make_async_copy(v_hbm, vbuf, in_sem.at[2]),
        pltpu.make_async_copy(x_hbm, h, in_sem.at[3]),
        pltpu.make_async_copy(wxp_hbm, wxp, in_sem.at[4]),
        pltpu.make_async_copy(wdt_hbm, wdt, in_sem.at[5]),
    ]
    for c in in_copies[:4]:
        c.start()
    for u in range(SLOTS):
        start(jnp.int32(u), u, u)
    for c in in_copies[4:]:
        c.start()
    for c in in_copies[:3]:
        c.wait()

    qi = lax.broadcasted_iota(jnp.int32, (seq, seq), 0)
    ki = lax.broadcasted_iota(jnp.int32, (seq, seq), 1)
    causal = jnp.concatenate([qi >= ki] * groups, axis=0)

    @pl.loop(0, kv_heads)
    def _(kvh):
        kcol = pl.ds(pl.multiple_of(kvh * 128, 128), 128)
        for b in range(n_seq):
            rs = pl.ds(b * seq, seq)
            kk = kbuf[rs, kcol]
            vv = vbuf[rs, kcol]
            qcols = [pl.ds(pl.multiple_of((kvh * groups + i) * 128, 128), 128) for i in range(groups)]
            qq = jnp.concatenate([qo[rs, c] for c in qcols], axis=0)
            s = lax.dot_general(qq, kk, (((1,), (1,)), ((), ())), preferred_element_type=F32) * 128 ** -0.5
            s = jnp.where(causal, s, -jnp.inf)
            e = jnp.exp(s - jnp.max(s, axis=-1, keepdims=True))
            p = (e * (1.0 / jnp.sum(e, axis=-1, keepdims=True))).astype(BF16)
            o = jnp.dot(p, vv, preferred_element_type=F32).astype(BF16)
            for i, c in enumerate(qcols):
                qo[rs, c] = o[i * seq:(i + 1) * seq]

    def norm_rows(g_idx):
        gain = norms[g_idx:g_idx + 1, :]

        @pl.loop(0, rows // 32)
        def _(i):
            rs = pl.ds(pl.multiple_of(i * 32, 32), 32)
            hv = h[rs, :].astype(F32)
            inv = lax.rsqrt(jnp.mean(hv * hv, axis=-1, keepdims=True) + EPS)
            a[rs, :] = (hv * inv * gain).astype(BF16)

    in_copies[3].wait()

    def wo_body(t, w0, w1):
        acc = jnp.dot(qo[:, :half_q], w0[...], preferred_element_type=F32)
        acc += jnp.dot(qo[:, half_q:], w1[...], preferred_element_type=F32)
        h[:, cols(t)] = (h[:, cols(t)].astype(F32) + acc).astype(BF16)

    phase(u_wo, dim // WN, wo_body)
    norm_rows(0)

    def gu_body(t, w0, w1):
        g = jnp.dot(a[...], w0[...], preferred_element_type=F32)
        u = jnp.dot(a[...], w1[...], preferred_element_type=F32)
        act[:, cols(t)] = (silu(g) * u).astype(BF16)

    phase(u_gu, ff // WN, gu_body)

    def dn_body(t, *ws):
        acc = None
        for (s, n), w in zip(chunks(ff), ws):
            d = jnp.dot(act[:, s:s + n], w[...], preferred_element_type=F32)
            acc = d if acc is None else acc + d
        h[:, cols(t)] = (h[:, cols(t)].astype(F32) + acc).astype(BF16)

    phase(u_dn, dim // WN, dn_body)
    norm_rows(1)

    row_id = lax.broadcasted_iota(jnp.int32, (seq, 1), 0)

    def scatter(dst, r0, t, val):
        for j in range(WN // 128):
            for i in range(seq // 8):
                dst[pl.ds((r0 + i * 8) * PITCH + t * (WN // 128) + j, 8, stride=PITCH), :] = (
                    val[i * 8:(i + 1) * 8, j * 128:(j + 1) * 128])

    def wx_body(t, w):
        res = jnp.dot(a[...], w[...], preferred_element_type=F32).astype(BF16).astype(F32)
        for b in range(n_seq):
            xi = res[b * seq:(b + 1) * seq]
            acc = chan[4:5, cols(t)] + chan[CONV - 1:CONV, cols(t)] * xi
            for j in range(CONV - 1):
                back = CONV - 1 - j
                prev = jnp.where(row_id >= back, pltpu.roll(xi, back, axis=0), 0.0)
                acc += chan[j:j + 1, cols(t)] * prev
            c = silu(acc).astype(BF16)
            xc[b * seq:(b + 1) * seq, cols(t)] = c
            scatter(xs, b * seq, t, c.astype(F32))

    phase(u_wx, inner // WN, wx_body)

    def wz_body(t, w):
        zg[:, cols(t)] = jnp.dot(a[...], w[...], preferred_element_type=F32).astype(BF16)

    phase(u_wz, inner // WN, wz_body)

    in_copies[4].wait()
    r = lax.dot_general(xc[...], wxp[...], (((1,), (1,)), ((), ())), preferred_element_type=F32)
    n_r = r.shape[1]
    col = lax.broadcasted_iota(jnp.int32, (1, n_r), 1)
    sq = r * r

    def inv_of(mask, n):
        return lax.rsqrt(jnp.sum(jnp.where(mask, sq, 0.0), axis=-1, keepdims=True) * (1.0 / n) + EPS)

    m_dt = col < dt_rank
    m_b = (col >= dt_rank) & (col < dt_rank + n_state)
    m_c = col >= dt_rank + n_state
    inv = jnp.where(m_dt, inv_of(m_dt, dt_rank), jnp.where(m_b, inv_of(m_b, n_state), inv_of(m_c, n_state)))
    rn = r * inv * gains[0:1, :]
    for n in range(n_state):
        bb[n * rows:(n + 1) * rows, :] = jnp.broadcast_to(rn[:, dt_rank + n:dt_rank + n + 1], (rows, 128))
        c0 = dt_rank + n_state + n
        cb[n * rows:(n + 1) * rows, :] = jnp.broadcast_to(rn[:, c0:c0 + 1], (rows, 128))
    dt_in = rn[:, :dt_rank].astype(BF16)
    a[:, :dt_rank] = dt_in
    in_copies[5].wait()

    @pl.loop(0, inner // WN)
    def _(t):
        pre = jnp.dot(a[:, :dt_rank], wdt[:, cols(t)], preferred_element_type=F32) + chan[5:6, cols(t)]
        step = jnp.maximum(pre, 0.0) + jnp.log1p(jnp.exp(-jnp.abs(pre)))
        for b in range(n_seq):
            scatter(delta, b * seq, t, step[b * seq:(b + 1) * seq])

    def bcast(ref, idx):
        return jnp.broadcast_to(ref[pl.ds(idx, 1), :], (8, 128))

    @pl.loop(0, n_seq)
    def _(b):
        @pl.loop(0, lanes // 8)
        def _(c):
            av = [a2[pl.ds(pl.multiple_of(n * lanes + c * 8, 8), 8), :] for n in range(n_state)]
            dsk = dskip[pl.ds(pl.multiple_of(c * 8, 8), 8), :]

            def step(i, st):
                st = list(st)
                for k in range(4):
                    r = b * seq + i * 4 + k
                    at = pl.ds(r * PITCH + c * 8, 8)
                    d = delta[at, :]
                    x = xs[at, :]
                    dx = d * x
                    terms = []
                    for n in range(n_state):
                        st[n] = jnp.exp2(d * av[n]) * st[n] + dx * bcast(bb, n * rows + r)
                        terms.append(st[n] * bcast(cb, n * rows + r))
                    terms.append(dsk * x)
                    while len(terms) > 1:
                        terms = [terms[m] + terms[m + 1] for m in range(0, len(terms) - 1, 2)] + (
                            [terms[-1]] if len(terms) % 2 else [])
                    delta[at, :] = terms[0]
                return tuple(st)

            lax.fori_loop(0, seq // 4, step, tuple(jnp.zeros((8, 128), F32) for _ in range(n_state)))

    @pl.loop(0, rows // 16)
    def _(i):
        r0 = pl.multiple_of(i * 16, 16)
        for j in range(lanes):
            y = jnp.concatenate([delta[pl.ds((r0 + 8 * m) * PITCH + j, 8, stride=PITCH), :] for m in range(2)], axis=0)
            z = zg[pl.ds(r0, 16), j * 128:(j + 1) * 128].astype(F32)
            act[pl.ds(r0, 16), j * 128:(j + 1) * 128] = (y * silu(z)).astype(BF16)

    def out_body(t, *ws):
        acc = None
        for (s, n), w in zip(chunks(inner), ws):
            d = jnp.dot(act[:, s:s + n], w[...], preferred_element_type=F32)
            acc = d if acc is None else acc + d
        out_ref[:, cols(t)] = (h[:, cols(t)].astype(F32) + acc).astype(BF16)

    phase(u_out, dim // WN, out_body)


def layer_pair(hidden, attn_norm, w_q, w_k, w_v, w_o, mlp_norm, w_gate, w_up, w_down, mamba_norm, w_in_x, w_in_z, conv_w, conv_b, w_xproj, dt_norm, b_norm, c_norm, w_dt, dt_bias, a_log, d_skip, w_out):
    dim = hidden.shape[-1]
    x = lax.all_to_all(hidden, "sp", 0, 1, tiled=True)
    n_seq, seq, _ = x.shape
    rows = n_seq * seq
    x = x.reshape(rows, dim)
    inner, n_state = a_log.shape
    normed = rms_scale(x, attn_norm).astype(BF16)

    def proj(w):
        return jnp.einsum("rd,dhk->rhk", normed, w, preferred_element_type=F32).astype(BF16).reshape(rows, -1)

    q, k, v = proj(w_q), proj(w_k), proj(w_v)
    lanes = inner // 128
    norms = jnp.stack([mlp_norm, mamba_norm]).astype(F32)
    chan = jnp.concatenate([conv_w.astype(F32), conv_b.astype(F32)[None], dt_bias[None], jnp.zeros((2, inner), F32)])
    gains = jnp.concatenate([dt_norm, b_norm, c_norm])[None]
    a2 = (-jnp.exp(a_log.T) * LOG2E).reshape(n_state * lanes, 128)
    dskip = d_skip.reshape(lanes, 128)
    hbm = pl.BlockSpec(memory_space=pltpu.HBM)
    vm = pl.BlockSpec(memory_space=pltpu.VMEM)
    out = pl.pallas_call(
        block_kernel,
        out_shape=jax.ShapeDtypeStruct((rows, dim), BF16),
        in_specs=[hbm] * 13 + [vm] * 5,
        out_specs=vm,
        scratch_shapes=[
            pltpu.VMEM((SLOTS, dim, WN), BF16),
            pltpu.VMEM(q.shape, BF16),
            pltpu.VMEM(k.shape, BF16),
            pltpu.VMEM(v.shape, BF16),
            pltpu.VMEM((rows, dim), BF16),
            pltpu.VMEM((rows, dim), BF16),
            pltpu.VMEM((rows, w_gate.shape[1]), BF16),
            pltpu.VMEM((rows, inner), BF16),
            pltpu.VMEM((rows, inner), BF16),
            pltpu.VMEM((rows * PITCH, 128), F32),
            pltpu.VMEM((rows * PITCH, 128), F32),
            pltpu.VMEM((rows * n_state, 128), F32),
            pltpu.VMEM((rows * n_state, 128), F32),
            pltpu.VMEM((w_xproj.shape[1], inner), BF16),
            pltpu.VMEM(w_dt.shape, BF16),
            pltpu.SemaphoreType.DMA((SLOTS,)),
            pltpu.SemaphoreType.DMA((6,)),
        ],
        compiler_params=pltpu.CompilerParams(vmem_limit_bytes=67043328),
        name="block",
    )(q, k, v, x, w_o.reshape(-1, dim), w_gate, w_up, w_down, w_in_x, w_in_z, w_xproj.T, w_dt, w_out,
      norms, chan, gains, dskip, a2)
    return lax.all_to_all(out.reshape(n_seq, seq, dim), "sp", 1, 0, tiled=True)


def solution(mesh):
    act_spec = P("dp", "sp", None)
    return jax.shard_map(
        layer_pair,
        mesh=mesh,
        in_specs=(act_spec,) + (P(),) * 23,
        out_specs=act_spec,
        check_vma=False,
    )
```

time: 983 us -> 231 us (0.23); the launches traced: 969 us -> 230 us
  waiting for transfers between devices: 250 us -> 0.01 us
  local copies, waits for them, and re-layouts: 289 us -> 54 us
  other arithmetic: 237 us -> 3.2 us
  matrix products: 163 us -> 18.7 us
  Pallas kernels: 0 us -> 129 us
  blocking collectives: 0 us -> 20.9 us
  between operations: 14.1 us -> 0.23 us
  starting transfers between devices: 14.6 us -> 4.33 us
    dynamic_update_slice x64 -> x0, local copies, waits for them, and re-layouts: 213 us -> none  [mamba_mixer(): lax.scan(local_step, zero_state, (step_size, x_conv, b_mat, c_mat))]
    reduce_sum x35 -> x0, other arithmetic: 202 us -> none  [the longest x16 97.8 us: carry_step(): return (ssm_state, jnp.sum(ssm_state * c_t[:, None, :], axis=-1))]
    all_gather x2 -> x0, waiting for transfers between devices: 193 us -> none  [the longest x1 193 us: mamba_mixer(): all_states = lax.all_gather(end_state, 'sp')]
    dot_general x13 -> x0, matrix products: 163 us -> none  [the longest x1 31.6 us: mamba_mixer(): jnp.einsum('tbe,ed->btd', gated_y, w_out, preferred_element_type=jnp.floa...]
    pallas_call x0 -> x1, Pallas kernels: none -> 129 us  [layer_pair(): pl.pallas_call(block_kernel, out_shape=jax.ShapeDtypeStruct((rows, dim),...]
    all_to_all x4 -> x1, waiting for transfers between devices: 55.3 us -> 0.01 us  [layer_pair(): x = lax.all_to_all(hidden, 'sp', 0, 1, tiled=True)]
    unnamed x46 -> x29, local copies, waits for them, and re-layouts: 7.07 us -> 44 us
    mul x64 -> x0, local copies, waits for them, and re-layouts: 32.3 us -> none  [the longest x16 16 us: local_step(): decay_t = jnp.exp(step_t[:, :, None] * a_mat)]
  transfers between devices with their start and end apart: 7 -> 1, of which waited for: 5 -> 0; matrix products, arithmetic and copies ran while one was open for 27% -> 20% of each run, Pallas kernels for 0% -> 0%
where the time goes in v1:
time: 231 us; the launch traced here: 230 us
  Pallas kernels  129 us (56%)
  local copies, waits for them, and re-layouts  54 us (23%)
  blocking collectives  20.9 us (9%)
  matrix products  18.7 us (8%)
  starting transfers between devices  4.33 us (2%)
  other arithmetic  3.2 us (1%)
    pallas_call x1, Pallas kernels, layer_pair(): pl.pallas_call(block_kernel, out_shape=jax.ShapeDtypeStruct((rows, dim),...  129 us
    unnamed x29, local copies, waits for them, and re-layouts  44 us
    all_to_all x1, blocking collectives, layer_pair(): return lax.all_to_all(out.reshape(n_seq, seq, dim), 'sp', 1, 0, tiled=True)  20.9 us
    unnamed x3, matrix products  18.7 us
    reshape x3, local copies, waits for them, and re-layouts, proj(): jnp.einsum('rd,dhk->rhk', normed, w, preferred_element_type=F32)  4.99 us
  transfers between devices with their start and end apart: 1, of which 0 were waited for; matrix products, arithmetic and copies ran while one was open for 20% of the time, Pallas kernels for 0%

profile of v1, /device:TPU:0, one launch (start us, length us, event | category | flops | bytes accessed | tf_op | source)
XLA Modules:
  0.0 229.9 jit_solution(10079158865839007766)
XLA Ops:
  0.0 4.3 %all-to-all-start = ((bf16[16,16,2560]{2,1,0:T(8,128)(2,1)}), bf16[16,16,2560]{2,1,0:T(8,128)(2,1)S(1)}, u32[]{:S(2)}, u32[]{:S(2)}) async-start(bf16[16,16,2560]{2,1,0:T(8,128)(2,1)} %param.24), calls=%async_computation | async-start | bytes 2621440 | tf_op jit(solution)/shard_map/all_to_all | solution.py:284
  4.4 0.0 copy-done.3
  4.4 0.1 multiply_bitcast_fusion
  4.5 0.0 copy-done.8
  4.5 0.6 maximum_convert_fusion.norms
  5.1 0.7 pad_maximum_fusion
  5.8 27.6 %copy.34 = bf16[2560,32,128]{0,2,1:T(8,128)(2,1)} copy(bf16[2560,32,128]{2,1,0:T(8,128)(2,1)} %param.26) | data formatting | bytes 41943040 | tf_op args[2]
  33.4 8.1 %copy.36 = bf16[2560,8,128]{0,2,1:T(8,128)(2,1)} copy(bf16[2560,8,128]{2,1,0:T(8,128)(2,1)} %param.27) | data formatting | bytes 10485760 | tf_op args[3]
  41.6 8.2 %copy.38 = bf16[2560,8,128]{0,2,1:T(8,128)(2,1)} copy(bf16[2560,8,128]{2,1,0:T(8,128)(2,1)} %param.28) | data formatting | bytes 10485760 | tf_op args[4]
  49.7 0.8 reshape.49.a2
  50.6 0.1 pad.6.clone
  50.6 0.7 maximum_maximum_fusion.chan
  51.4 0.0 all-to-all-done
  51.4 0.1 copy.33
  51.5 0.3 multiply_reduce_fusion
  51.8 0.1 rsqrt.12
  51.9 0.4 multiply_convert_fusion
  52.3 0.0 copy-start.1
  52.3 10.7 %fusion = f32[256,4096]{0,1:S(1)} fusion(bf16[256,2560]{1,0:T(8,128)(2,1)S(1)} %multiply_convert_fusion, bf16[2560,4096]{0,1:T(8,128)(2,1)} %bitcast.34), kind=kOutput, calls=%fused_computation.7 | convolution fusion | flops 5368709120 | bytes 26476544
  63.0 0.3 convert_element_type.32
  63.3 0.0 copy-start.2
  63.3 3.0 %copy.42.q_hbm = bf16[256,4096]{1,0:T(8,128)(2,1)} copy(bf16[256,4096]{0,1:T(8,128)(2,1)S(1)} %bitcast.39) | data formatting | bytes 4194304 | tf_op jit(solution)/shard_map/reshape | solution.py:292
  66.3 4.0 %fusion.1 = f32[256,1024]{0,1:S(1)} fusion(bf16[256,2560]{1,0:T(8,128)(2,1)S(1)} %copy-done.2, bf16[2560,1024]{0,1:T(8,128)(2,1)} %bitcast.41), kind=kOutput, calls=%fused_computation.8 | convolution fusion | flops 1342177280 | bytes 7602176
  70.3 0.1 convert_element_type.33
  70.4 1.0 copy.43.k_hbm
  71.4 4.0 %fusion.2 = f32[256,1024]{0,1:S(1)} fusion(bf16[256,2560]{1,0:T(8,128)(2,1)S(1)} %copy-done.2, bf16[2560,1024]{0,1:T(8,128)(2,1)} %bitcast.40), kind=kOutput, calls=%fused_computation.9 | convolution fusion | flops 1342177280 | bytes 7602176
  75.4 0.1 convert_element_type.34
  75.5 1.0 copy.44.v_hbm
  76.5 128.6 %block.1 = bf16[256,2560]{1,0:T(8,128)(2,1)} custom-call(bf16[256,4096]{1,0:T(8,128)(2,1)} %copy.42.q_hbm, bf16[256,1024]{1,0:T(8,128)(2,1)} %copy.43.k_hbm, bf16[256,1024]{1,0:T(8,128)(2,1)} %copy.44.v_hbm, bf16[256,2560]{1,0:T(8,128)(2,1)} %bitcast.38, bf16[4096,2560]{1,0:T(8,128)(2,1)} %bitcast.35, bf16[2560,9728]{1,0:T(8,128)(2,1)} %wg.1, ...), custom_call_target="tpu_custom_call" | custom-call | tf_op jit(solution)/shard_map/block/pallas_call | solution.py:303
  205.1 2.7 %copy.40 = bf16[2,128,2560]{2,0,1:T(2,128)(2,1)S(1)} copy(bf16[2,128,2560]{2,1,0:T(8,128)(2,1)} %bitcast.43) | data formatting | bytes 2621440 | tf_op jit(solution)/shard_map/reshape | solution.py:331
  207.8 20.9 %all_to_all.33 = bf16[2,128,2560]{2,0,1:T(2,128)(2,1)S(1)} all-to-all(bf16[2,128,2560]{2,0,1:T(2,128)(2,1)S(1)} %copy.40), channel_id=1, replica_groups=mesh['dp'=1,'sp'=8] {'sp'}, dimensions={1} | all-to-all | bytes 2621440 | tf_op jit(solution)/shard_map/all_to_all | solution.py:331
  228.6 1.3 copy.41
  (29 shorter events, 0.1 us)
Async XLA Ops:
  0.0 4.4 %copy-start.3 = (f32[5120,16]{0,1:T(8,128)S(1)}, f32[5120,16]{0,1:T(8,128)}, u32[]{:S(2)}) copy-start(f32[5120,16]{0,1:T(8,128)} %param.45) | copy-start | bytes 983044
  0.0 4.4 %copy-start.7 = (bf16[2560]{0:T(1024)(128)(2,1)S(1)}, bf16[2560]{0:T(1024)(128)(2,1)}, u32[]{:S(2)}) copy-start(bf16[2560]{0:T(1024)(128)(2,1)} %param.34) | copy-start | bytes 15364
  0.0 4.4 %copy-start.8 = (bf16[2560]{0:T(1024)(128)(2,1)S(1)}, bf16[2560]{0:T(1024)(128)(2,1)}, u32[]{:S(2)}) copy-start(bf16[2560]{0:T(1024)(128)(2,1)} %param.30) | copy-start | bytes 15364
  0.0 5.1 %copy-start.10 = (f32[160]{0:T(256)S(1)}, f32[160]{0:T(256)}, u32[]{:S(2)}) copy-start(f32[160]{0:T(256)} %param.40) | copy-start | bytes 1924
  0.0 5.1 %copy-start.12 = (f32[16]{0:T(128)S(1)}, f32[16]{0:T(128)}, u32[]{:S(2)}) copy-start(f32[16]{0:T(128)} %param.41) | copy-start | bytes 196
  0.0 5.1 %copy-start.11 = (f32[16]{0:T(128)S(1)}, f32[16]{0:T(128)}, u32[]{:S(2)}) copy-start(f32[16]{0:T(128)} %param.42) | copy-start | bytes 196
  0.0 5.8 %copy-start.9 = (bf16[2560]{0:T(1024)(128)(2,1)S(1)}, bf16[2560]{0:T(1024)(128)(2,1)}, u32[]{:S(2)}) copy-start(bf16[2560]{0:T(1024)(128)(2,1)} %param.25) | copy-start | bytes 15364
  0.0 51.3 %all-to-all-start = ((bf16[16,16,2560]{2,1,0:T(8,128)(2,1)}), bf16[16,16,2560]{2,1,0:T(8,128)(2,1)S(1)}, u32[]{:S(2)}, u32[]{:S(2)}) async-start(bf16[16,16,2560]{2,1,0:T(8,128)(2,1)} %param.24), calls=%async_computation | async-start | bytes 2621440 | tf_op jit(solution)/shard_map/all_to_all | solution.py:284
  41.5 9.0 %copy-start.4 = (bf16[4,5120]{1,0:T(4,128)(2,1)S(1)}, bf16[4,5120]{1,0:T(4,128)(2,1)}, u32[]{:S(2)}) copy-start(bf16[4,5120]{1,0:T(4,128)(2,1)} %param.37) | copy-start | bytes 122884
  41.6 9.0 %copy-start.6 = (bf16[5120]{0:T(1024)(128)(2,1)S(1)}, bf16[5120]{0:T(1024)(128)(2,1)}, u32[]{:S(2)}) copy-start(bf16[5120]{0:T(1024)(128)(2,1)} %param.38) | copy-start | bytes 30724
  41.6 9.1 %copy-start.5 = (f32[5120]{0:T(1024)S(1)}, f32[5120]{0:T(1024)}, u32[]{:S(2)}) copy-start(f32[5120]{0:T(1024)} %param.44) | copy-start | bytes 61444
  51.5 11.5 %copy-start = (bf16[8,2,16,2560]{3,2,0,1:T(8,128)(2,1)}, bf16[8,2,16,2560]{3,2,0,1:T(8,128)(2,1)S(1)}, u32[]{:S(2)}) copy-start(bf16[8,2,16,2560]{3,2,0,1:T(8,128)(2,1)S(1)} %copy.33) | copy-start | bytes 3932164
  52.3 10.7 %copy-start.1 = (bf16[256,2560]{1,0:T(8,128)(2,1)}, bf16[256,2560]{1,0:T(8,128)(2,1)S(1)}, u32[]{:S(2)}) copy-start(bf16[256,2560]{1,0:T(8,128)(2,1)S(1)} %multiply_convert_fusion) | copy-start | bytes 3932164
  63.3 3.0 %copy-start.2 = (bf16[256,2560]{1,0:T(8,128)(2,1)S(1)}, bf16[256,2560]{1,0:T(8,128)(2,1)}, u32[]{:S(2)}) copy-start(bf16[256,2560]{1,0:T(8,128)(2,1)} %copy-done.1) | copy-start | bytes 3932164

commit v2 on v1

--- a/solution.py
+++ b/solution.py
@@ -9,7 +9,9 @@
 
 EPS = 1e-6
 CONV = 4
-SLOTS = 9
+SLOTS = 12
+STAGE = 4
+KB = 64
 WN = 512
 PITCH = 41
 F32 = jnp.float32
@@ -28,18 +30,21 @@
     return half + half * jnp.tanh(half)
 
 
-def block_kernel(q_hbm, k_hbm, v_hbm, x_hbm, wo, wg, wu, wd, wx, wz, wxp_hbm, wdt_hbm, wout,
+def block_kernel(x_hbm, wq, wk, wv, wo, wg, wu, wd, wx, wz, wxp_hbm, wdt_hbm, wout,
                  norms, chan, gains, dskip, a2, out_ref,
-                 ring, qo, kbuf, vbuf, h, a, act, xc, zg, delta, xs, bb, cb, wxp, wdt,
-                 ring_sem, in_sem):
+                 ring, stage, tmp, qkv, h, a, act, delta, xs, bb, cb, wxp, wdt,
+                 ring_sem, stage_sem, in_sem, send_sem, recv_sem):
     rows, dim = h.shape
-    seq = 128
-    n_seq = rows // seq
+    n_seq, seq = 2, 128
+    n_dev = x_hbm.shape[0] // n_seq
+    tok = x_hbm.shape[1]
+    me = lax.axis_index("sp")
     inner = wx.shape[1]
     ff = wg.shape[1]
     qdim = wo.shape[0]
-    kv_heads = kbuf.shape[1] // 128
-    groups = qdim // kbuf.shape[1]
+    heads = qdim // 128
+    kv_heads = (qkv.shape[1] - qdim) // 256
+    groups = heads // kv_heads
     lanes = inner // 128
     n_state = a2.shape[0] // lanes
     dt_rank = wdt.shape[0]
@@ -62,6 +67,7 @@
         return first
 
     half_q = qdim // 2
+    u_qkv = add_seg(qkv.shape[1] // WN, [(None, 0, dim)])
     u_wo = add_seg(dim // WN, [(wo, 0, half_q), (wo, half_q, half_q)])
     u_gu = add_seg(ff // WN, [(wg, 0, dim), (wu, 0, dim)])
     u_dn = add_seg(dim // WN, [(wd, s, n) for s, n in chunks(ff)])
@@ -75,7 +81,7 @@
 
     def start(u, lo, hi):
         for first, last, parts in segs:
-            if hi < first or lo >= last:
+            if hi < first or lo >= last or parts[0][0] is None:
                 continue
             n = len(parts)
             for i, part in enumerate(parts):
@@ -92,28 +98,106 @@
             vals = []
             for i, part in enumerate(parts):
                 slot = lax.rem(first + t * n + i, SLOTS)
-                copy(part, 0, slot).wait()
+                if part[0] is not None:
+                    copy(part, 0, slot).wait()
                 vals.append(ring.at[slot, pl.ds(0, part[2])])
             body(t, *vals)
             for i in range(n):
                 start(first + t * n + i + SLOTS, first + SLOTS, first + SLOTS + n_tiles * n - 1)
 
+    def norm_rows(g_idx):
+        gain = norms[g_idx:g_idx + 1, :]
+
+        @pl.loop(0, rows // 32)
+        def _(i):
+            rs = pl.ds(pl.multiple_of(i * 32, 32), 32)
+            hv = h[rs, :].astype(F32)
+            inv = lax.rsqrt(jnp.mean(hv * hv, axis=-1, keepdims=True) + EPS)
+            a[rs, :] = (hv * inv * gain).astype(BF16)
+
     in_copies = [
-        pltpu.make_async_copy(q_hbm, qo, in_sem.at[0]),
-        pltpu.make_async_copy(k_hbm, kbuf, in_sem.at[1]),
-        pltpu.make_async_copy(v_hbm, vbuf, in_sem.at[2]),
-        pltpu.make_async_copy(x_hbm, h, in_sem.at[3]),
-        pltpu.make_async_copy(wxp_hbm, wxp, in_sem.at[4]),
-        pltpu.make_async_copy(wdt_hbm, wdt, in_sem.at[5]),
+        pltpu.make_async_copy(wxp_hbm, wxp, in_sem.at[0]),
+        pltpu.make_async_copy(wdt_hbm, wdt, in_sem.at[1]),
     ]
-    for c in in_copies[:4]:
+    n_q = wq.shape[0] // KB
+    n_kv = wk.shape[0] // KB
+
+    def stage_copy(w, c, slot):
+        return pltpu.make_async_copy(w.at[pl.ds(c * KB, KB)], stage.at[slot], stage_sem.at[slot])
+
+    def stage_start(i):
+        slot = lax.rem(i, STAGE)
+        for w, lo, n in ((wq, 0, n_q), (wk, n_q, n_kv), (wv, n_q + n_kv, n_kv)):
+            @pl.when((i >= lo) & (i < lo + n))
+            def _(w=w, lo=lo):
+                stage_copy(w, i - lo, slot).start()
+
+    for i in range(STAGE):
+        stage_start(jnp.int32(i))
+
+    barrier = pltpu.get_barrier_semaphore()
+    for d in range(1, n_dev):
+        pl.semaphore_signal(barrier, inc=1, device_id={"sp": lax.rem(me + d, n_dev)}, device_id_type=pl.DeviceIdType.MESH)
+    pl.semaphore_wait(barrier, n_dev - 1)
+
+    def exchange(src_of, dst_of, ex):
+        for d in range(1, n_dev):
+            peer = lax.rem(me + d, n_dev)
+            for b in range(n_seq):
+                pltpu.make_async_remote_copy(
+                    src_ref=src_of(peer, b), dst_ref=dst_of(me, b), send_sem=send_sem.at[ex], recv_sem=recv_sem.at[ex],
+                    device_id={"sp": peer}, device_id_type=pl.DeviceIdType.MESH).start()
+        for b in range(n_seq):
+            pltpu.make_async_copy(src_of(me, b), dst_of(me, b), recv_sem.at[ex]).start()
+
+    def exchange_wait(whole_dst, part_src, ex):
+        pltpu.make_async_copy(whole_dst, whole_dst, recv_sem.at[ex]).wait()
+        pltpu.make_async_copy(part_src, part_src, send_sem.at[ex]).wait()
+
+    def blk(owner, b):
+        return pl.ds(pl.multiple_of(b * seq + owner * tok, tok), tok)
+
+    exchange(lambda p, b: x_hbm.at[p * n_seq + b], lambda p, b: h.at[blk(p, b)], 0)
+    for c in in_copies:
         c.start()
-    for u in range(SLOTS):
-        start(jnp.int32(u), u, u)
-    for c in in_copies[4:]:
-        c.start()
-    for c in in_copies[:3]:
-        c.wait()
+
+    def relayout(i, n_heads, unit0, k0):
+        slot = lax.rem(i, STAGE)
+        per = 32 // n_heads
+        pitch = n_heads + 1
+        stage_copy(wq, 0, slot).wait()
+
+        @pl.loop(0, KB * per // 16)
+        def _(g):
+            buf = tmp.at[lax.rem(g, 2)]
+            for r in range(16 // per):
+                val = stage[slot, g * (16 // per) + r].astype(F32)
+                for j in range(per):
+                    buf[pl.ds((r * per + j) * pitch, n_heads), :] = val[j * n_heads:(j + 1) * n_heads]
+            ks = pl.ds(pl.multiple_of(k0 + g * 16, 16), 16)
+            for hd in range(n_heads):
+                w = WN // 128
+                ring[unit0 + hd // w, ks, (hd % w) * 128:(hd % w + 1) * 128] = (
+                    buf[pl.ds(hd, 16, stride=pitch), :].astype(BF16))
+
+        stage_start(i + STAGE)
+
+    @pl.loop(0, n_q)
+    def _(i):
+        relayout(i, heads, 0, i * KB)
+
+    for m in range(2):
+        @pl.loop(0, n_kv)
+        def _(i, m=m):
+            relayout(n_q + m * n_kv + i, kv_heads, (qdim + m * kv_heads * 128) // WN, i * KB * (32 // kv_heads))
+
+    exchange_wait(h, h.at[pl.ds(0, rows - n_seq * tok)], 0)
+    norm_rows(0)
+
+    def qkv_body(t, w):
+        qkv[:, cols(t)] = jnp.dot(a[...], w[...], preferred_element_type=F32).astype(BF16)
+
+    phase(u_qkv, qkv.shape[1] // WN, qkv_body)
 
     qi = lax.broadcasted_iota(jnp.int32, (seq, seq), 0)
     ki = lax.broadcasted_iota(jnp.int32, (seq, seq), 1)
@@ -121,40 +205,27 @@
 
     @pl.loop(0, kv_heads)
     def _(kvh):
-        kcol = pl.ds(pl.multiple_of(kvh * 128, 128), 128)
         for b in range(n_seq):
             rs = pl.ds(b * seq, seq)
-            kk = kbuf[rs, kcol]
-            vv = vbuf[rs, kcol]
+            kk = qkv[rs, pl.ds(pl.multiple_of(qdim + kvh * 128, 128), 128)]
+            vv = qkv[rs, pl.ds(pl.multiple_of(qdim + (kv_heads + kvh) * 128, 128), 128)]
             qcols = [pl.ds(pl.multiple_of((kvh * groups + i) * 128, 128), 128) for i in range(groups)]
-            qq = jnp.concatenate([qo[rs, c] for c in qcols], axis=0)
+            qq = jnp.concatenate([qkv[rs, c] for c in qcols], axis=0)
             s = lax.dot_general(qq, kk, (((1,), (1,)), ((), ())), preferred_element_type=F32) * 128 ** -0.5
             s = jnp.where(causal, s, -jnp.inf)
             e = jnp.exp(s - jnp.max(s, axis=-1, keepdims=True))
             p = (e * (1.0 / jnp.sum(e, axis=-1, keepdims=True))).astype(BF16)
             o = jnp.dot(p, vv, preferred_element_type=F32).astype(BF16)
             for i, c in enumerate(qcols):
-                qo[rs, c] = o[i * seq:(i + 1) * seq]
-
-    def norm_rows(g_idx):
-        gain = norms[g_idx:g_idx + 1, :]
-
-        @pl.loop(0, rows // 32)
-        def _(i):
-            rs = pl.ds(pl.multiple_of(i * 32, 32), 32)
-            hv = h[rs, :].astype(F32)
-            inv = lax.rsqrt(jnp.mean(hv * hv, axis=-1, keepdims=True) + EPS)
-            a[rs, :] = (hv * inv * gain).astype(BF16)
-
-    in_copies[3].wait()
+                qkv[rs, c] = o[i * seq:(i + 1) * seq]
 
     def wo_body(t, w0, w1):
-        acc = jnp.dot(qo[:, :half_q], w0[...], preferred_element_type=F32)
-        acc += jnp.dot(qo[:, half_q:], w1[...], preferred_element_type=F32)
+        acc = jnp.dot(qkv[:, :half_q], w0[...], preferred_element_type=F32)
+        acc += jnp.dot(qkv[:, half_q:qdim], w1[...], preferred_element_type=F32)
         h[:, cols(t)] = (h[:, cols(t)].astype(F32) + acc).astype(BF16)
 
     phase(u_wo, dim // WN, wo_body)
-    norm_rows(0)
+    norm_rows(1)
 
     def gu_body(t, w0, w1):
         g = jnp.dot(a[...], w0[...], preferred_element_type=F32)
@@ -171,7 +242,7 @@
         h[:, cols(t)] = (h[:, cols(t)].astype(F32) + acc).astype(BF16)
 
     phase(u_dn, dim // WN, dn_body)
-    norm_rows(1)
+    norm_rows(2)
 
     row_id = lax.broadcasted_iota(jnp.int32, (seq, 1), 0)
 
@@ -191,18 +262,18 @@
                 prev = jnp.where(row_id >= back, pltpu.roll(xi, back, axis=0), 0.0)
                 acc += chan[j:j + 1, cols(t)] * prev
             c = silu(acc).astype(BF16)
-            xc[b * seq:(b + 1) * seq, cols(t)] = c
+            act[b * seq:(b + 1) * seq, cols(t)] = c
             scatter(xs, b * seq, t, c.astype(F32))
 
     phase(u_wx, inner // WN, wx_body)
 
     def wz_body(t, w):
-        zg[:, cols(t)] = jnp.dot(a[...], w[...], preferred_element_type=F32).astype(BF16)
+        qkv[:, cols(t)] = jnp.dot(a[...], w[...], preferred_element_type=F32).astype(BF16)
 
     phase(u_wz, inner // WN, wz_body)
 
-    in_copies[4].wait()
-    r = lax.dot_general(xc[...], wxp[...], (((1,), (1,)), ((), ())), preferred_element_type=F32)
+    in_copies[0].wait()
+    r = lax.dot_general(act[:, :inner], wxp[...], (((1,), (1,)), ((), ())), preferred_element_type=F32)
     n_r = r.shape[1]
     col = lax.broadcasted_iota(jnp.int32, (1, n_r), 1)
     sq = r * r
@@ -221,7 +292,7 @@
         cb[n * rows:(n + 1) * rows, :] = jnp.broadcast_to(rn[:, c0:c0 + 1], (rows, 128))
     dt_in = rn[:, :dt_rank].astype(BF16)
     a[:, :dt_rank] = dt_in
-    in_copies[5].wait()
+    in_copies[1].wait()
 
     @pl.loop(0, inner // WN)
     def _(t):
@@ -266,7 +337,7 @@
         r0 = pl.multiple_of(i * 16, 16)
         for j in range(lanes):
             y = jnp.concatenate([delta[pl.ds((r0 + 8 * m) * PITCH + j, 8, stride=PITCH), :] for m in range(2)], axis=0)
-            z = zg[pl.ds(r0, 16), j * 128:(j + 1) * 128].astype(F32)
+            z = qkv[pl.ds(r0, 16), j * 128:(j + 1) * 128].astype(F32)
             act[pl.ds(r0, 16), j * 128:(j + 1) * 128] = (y * silu(z)).astype(BF16)
 
     def out_body(t, *ws):
@@ -274,47 +345,40 @@
         for (s, n), w in zip(chunks(inner), ws):
             d = jnp.dot(act[:, s:s + n], w[...], preferred_element_type=F32)
             acc = d if acc is None else acc + d
-        out_ref[:, cols(t)] = (h[:, cols(t)].astype(F32) + acc).astype(BF16)
+        a[:, cols(t)] = (h[:, cols(t)].astype(F32) + acc).astype(BF16)
+        exchange(lambda p, b: a.at[blk(p, b), cols(t)], lambda p, b: out_ref.at[p * n_seq + b, :, cols(t)], 1)
 
     phase(u_out, dim // WN, out_body)
+    exchange_wait(out_ref, a.at[pl.ds(0, rows - n_seq * tok)], 1)
 
 
 def layer_pair(hidden, attn_norm, w_q, w_k, w_v, w_o, mlp_norm, w_gate, w_up, w_down, mamba_norm, w_in_x, w_in_z, conv_w, conv_b, w_xproj, dt_norm, b_norm, c_norm, w_dt, dt_bias, a_log, d_skip, w_out):
-    dim = hidden.shape[-1]
-    x = lax.all_to_all(hidden, "sp", 0, 1, tiled=True)
-    n_seq, seq, _ = x.shape
-    rows = n_seq * seq
-    x = x.reshape(rows, dim)
+    n_batch, tok, dim = hidden.shape
+    n_seq = n_batch // lax.axis_size("sp")
+    rows = n_batch * tok
     inner, n_state = a_log.shape
-    normed = rms_scale(x, attn_norm).astype(BF16)
-
-    def proj(w):
-        return jnp.einsum("rd,dhk->rhk", normed, w, preferred_element_type=F32).astype(BF16).reshape(rows, -1)
-
-    q, k, v = proj(w_q), proj(w_k), proj(w_v)
     lanes = inner // 128
-    norms = jnp.stack([mlp_norm, mamba_norm]).astype(F32)
+    norms = jnp.stack([attn_norm, mlp_norm, mamba_norm]).astype(F32)
     chan = jnp.concatenate([conv_w.astype(F32), conv_b.astype(F32)[None], dt_bias[None], jnp.zeros((2, inner), F32)])
     gains = jnp.concatenate([dt_norm, b_norm, c_norm])[None]
     a2 = (-jnp.exp(a_log.T) * LOG2E).reshape(n_state * lanes, 128)
     dskip = d_skip.reshape(lanes, 128)
     hbm = pl.BlockSpec(memory_space=pltpu.HBM)
     vm = pl.BlockSpec(memory_space=pltpu.VMEM)
-    out = pl.pallas_call(
+    qkv_dim = (w_q.shape[1] + w_k.shape[1] + w_v.shape[1]) * 128
+    return pl.pallas_call(
         block_kernel,
-        out_shape=jax.ShapeDtypeStruct((rows, dim), BF16),
+        out_shape=jax.ShapeDtypeStruct(hidden.shape, BF16),
         in_specs=[hbm] * 13 + [vm] * 5,
-        out_specs=vm,
+        out_specs=hbm,
         scratch_shapes=[
             pltpu.VMEM((SLOTS, dim, WN), BF16),
-            pltpu.VMEM(q.shape, BF16),
-            pltpu.VMEM(k.shape, BF16),
-            pltpu.VMEM(v.shape, BF16),
+            pltpu.VMEM((STAGE, KB, 32, 128), BF16),
+            pltpu.VMEM((2, 16 * 33, 128), F32),
+            pltpu.VMEM((rows, qkv_dim), BF16),
             pltpu.VMEM((rows, dim), BF16),
             pltpu.VMEM((rows, dim), BF16),
             pltpu.VMEM((rows, w_gate.shape[1]), BF16),
-            pltpu.VMEM((rows, inner), BF16),
-            pltpu.VMEM((rows, inner), BF16),
             pltpu.VMEM((rows * PITCH, 128), F32),
             pltpu.VMEM((rows * PITCH, 128), F32),
             pltpu.VMEM((rows * n_state, 128), F32),
@@ -322,13 +386,15 @@
             pltpu.VMEM((w_xproj.shape[1], inner), BF16),
             pltpu.VMEM(w_dt.shape, BF16),
             pltpu.SemaphoreType.DMA((SLOTS,)),
-            pltpu.SemaphoreType.DMA((6,)),
+            pltpu.SemaphoreType.DMA((STAGE,)),
+            pltpu.SemaphoreType.DMA((2,)),
+            pltpu.SemaphoreType.DMA((2,)),
+            pltpu.SemaphoreType.DMA((2,)),
         ],
-        compiler_params=pltpu.CompilerParams(vmem_limit_bytes=67043328),
+        compiler_params=pltpu.CompilerParams(vmem_limit_bytes=67043328, collective_id=0, has_side_effects=True),
         name="block",
-    )(q, k, v, x, w_o.reshape(-1, dim), w_gate, w_up, w_down, w_in_x, w_in_z, w_xproj.T, w_dt, w_out,
-      norms, chan, gains, dskip, a2)
-    return lax.all_to_all(out.reshape(n_seq, seq, dim), "sp", 1, 0, tiled=True)
+    )(hidden, w_q.reshape(-1, 32, 128), w_k.reshape(-1, 32, 128), w_v.reshape(-1, 32, 128), w_o.reshape(-1, dim),
+      w_gate, w_up, w_down, w_in_x, w_in_z, w_xproj.T, w_dt, w_out, norms, chan, gains, dskip, a2)
 
 
 def solution(mesh):

time: 231 us -> 179 us (0.77)
  local copies, waits for them, and re-layouts: 54 us -> 5.41 us
  Pallas kernels: 129 us -> 167 us
  blocking collectives: 20.9 us -> 0 us
  matrix products: 18.7 us -> 0 us
  starting transfers between devices: 4.33 us -> 0 us
  other arithmetic: 3.2 us -> 6 us
    unnamed x29 -> x1, local copies, waits for them, and re-layouts: 44 us -> 2.46 us
    pallas_call x1, Pallas kernels: 129 us -> 167 us  [layer_pair(): pl.pallas_call(block_kernel, out_shape=jax.ShapeDtypeStruct(hidden.shape,...]
    all_to_all x1 -> x0, blocking collectives: 20.9 us -> none  [layer_pair(): return lax.all_to_all(out.reshape(n_seq, seq, dim), 'sp', 1, 0, tiled=True)]
    unnamed x3 -> x0, matrix products: 18.7 us -> none
    reshape x4 -> x0, local copies, waits for them, and re-layouts: 7.66 us -> none  [the longest x3 4.99 us: proj(): jnp.einsum('rd,dhk->rhk', normed, w, preferred_element_type=F32)]
    all_to_all x1 -> x0, starting transfers between devices: 4.33 us -> none  [layer_pair(): x = lax.all_to_all(hidden, 'sp', 0, 1, tiled=True)]
  transfers between devices with their start and end apart: 1 -> 0, of which waited for: 0 -> 0; matrix products, arithmetic and copies ran while one was open for 20% -> 0% of each run, Pallas kernels for 0% -> 0%
where the time goes in v2:
time: 179 us
  Pallas kernels  167 us (93%)
  other arithmetic  6 us (3%)
  local copies, waits for them, and re-layouts  5.41 us (3%)
    pallas_call x1, Pallas kernels, layer_pair(): pl.pallas_call(block_kernel, out_shape=jax.ShapeDtypeStruct(hidden.shape,...  167 us

profile of v2, /device:TPU:0, one launch (start us, length us, event | category | flops | bytes accessed | tf_op | source)
XLA Modules:
  0.0 178.5 jit_solution(1443508185164662021)
XLA Ops:
  0.0 0.1 pad.6.clone
  0.1 1.4 pad_maximum_fusion
  1.4 0.7 stack.12
  2.1 0.7 stack.13
  2.8 0.7 stack.14
  3.5 0.7 maximum_convert_fusion.norms
  4.2 0.7 broadcast_in_dim.20
  4.9 0.8 convert_element_type.8
  5.7 1.5 maximum_maximum_fusion.chan
  7.2 1.0 multiply_bitcast_fusion
  8.2 0.8 reshape.19.a2
  9.0 167.1 %block.1 = bf16[16,16,2560]{2,1,0:T(8,128)(2,1)} custom-call(bf16[16,16,2560]{2,1,0:T(8,128)(2,1)} %x_hbm.1, bf16[2560,32,128]{2,1,0:T(8,128)(2,1)} %wq.1, bf16[640,32,128]{2,1,0:T(8,128)(2,1)} %bitcast.11, bf16[640,32,128]{2,1,0:T(8,128)(2,1)} %bitcast.12, bf16[4096,2560]{1,0:T(8,128)(2,1)} %bitcast.10, bf16[2560,9728]{1,0:T(8,128)(2,1)} %wg.1, ...), custom_call_target="tpu_custom_call" | custom-call | tf_op jit(solution)/shard_map/block/pallas_call | solution.py:369
  176.1 2.5 %copy.26 = bf16[16,16,2560]{2,1,0:T(8,128)(2,1)} copy(bf16[16,16,2560]{2,1,0:T(8,128)(2,1)} %block.1) | data formatting | bytes 2621440
  (1 shorter events, 0.0 us)

commit v3 on v2

--- a/solution.py
+++ b/solution.py
@@ -10,7 +10,7 @@
 EPS = 1e-6
 CONV = 4
 SLOTS = 12
-STAGE = 4
+STAGE = 6
 KB = 64
 WN = 512
 PITCH = 41
@@ -31,8 +31,8 @@
 
 
 def block_kernel(x_hbm, wq, wk, wv, wo, wg, wu, wd, wx, wz, wxp_hbm, wdt_hbm, wout,
-                 norms, chan, gains, dskip, a2, out_ref,
-                 ring, stage, tmp, qkv, h, a, act, delta, xs, bb, cb, wxp, wdt,
+                 attn_g, mlp_g, mamba_g, conv_w, conv_b, dt_g, b_g, c_g, dt_b, dskip, a_log, out_ref,
+                 ring, stage, acc_ref, qkv, h, a, act, delta, xs, bb, cb, wxp, wdt, a2, chan, rn_ref,
                  ring_sem, stage_sem, in_sem, send_sem, recv_sem):
     rows, dim = h.shape
     n_seq, seq = 2, 128
@@ -46,7 +46,7 @@
     kv_heads = (qkv.shape[1] - qdim) // 256
     groups = heads // kv_heads
     lanes = inner // 128
-    n_state = a2.shape[0] // lanes
+    n_state = a_log.shape[0]
     dt_rank = wdt.shape[0]
     unit = ring.shape[1]
 
@@ -89,24 +89,32 @@
                 def _(part=part, first=first, n=n):
                     copy(part, lax.div(u - first, n), lax.rem(u, SLOTS)).start()
 
-    def phase(first, n_tiles, body):
+    def phase(first, n_tiles, body, per=1):
         parts = [s for s in segs if s[0] == first][0][2]
         n = len(parts)
 
-        @pl.loop(0, n_tiles)
-        def _(t):
-            vals = []
-            for i, part in enumerate(parts):
-                slot = lax.rem(first + t * n + i, SLOTS)
+        def group(t0, count):
+            views = []
+            for u in range(count * n):
+                slot = lax.rem(first + t0 * n + u, SLOTS)
+                part = parts[u % n]
                 if part[0] is not None:
                     copy(part, 0, slot).wait()
-                vals.append(ring.at[slot, pl.ds(0, part[2])])
-            body(t, *vals)
-            for i in range(n):
-                start(first + t * n + i + SLOTS, first + SLOTS, first + SLOTS + n_tiles * n - 1)
-
-    def norm_rows(g_idx):
-        gain = norms[g_idx:g_idx + 1, :]
+                views.append(ring.at[slot, pl.ds(0, part[2])])
+            for m in range(count):
+                body(t0 + m, *views[m * n:(m + 1) * n])
+            for u in range(count * n):
+                start(first + t0 * n + u + SLOTS, first + SLOTS, first + SLOTS + n_tiles * n - 1)
+
+        @pl.loop(0, n_tiles // per)
+        def _(g):
+            group(g * per, per)
+
+        if n_tiles % per:
+            group(jnp.int32(n_tiles - n_tiles % per), n_tiles % per)
+
+    def norm_rows(g_ref):
+        gain = g_ref[...].astype(F32).reshape(1, dim)
 
         @pl.loop(0, rows // 32)
         def _(i):
@@ -140,14 +148,14 @@
         pl.semaphore_signal(barrier, inc=1, device_id={"sp": lax.rem(me + d, n_dev)}, device_id_type=pl.DeviceIdType.MESH)
     pl.semaphore_wait(barrier, n_dev - 1)
 
-    def exchange(src_of, dst_of, ex):
+    def exchange(src_of, dst_of, ex, bs):
         for d in range(1, n_dev):
             peer = lax.rem(me + d, n_dev)
-            for b in range(n_seq):
+            for b in bs:
                 pltpu.make_async_remote_copy(
                     src_ref=src_of(peer, b), dst_ref=dst_of(me, b), send_sem=send_sem.at[ex], recv_sem=recv_sem.at[ex],
                     device_id={"sp": peer}, device_id_type=pl.DeviceIdType.MESH).start()
-        for b in range(n_seq):
+        for b in bs:
             pltpu.make_async_copy(src_of(me, b), dst_of(me, b), recv_sem.at[ex]).start()
 
     def exchange_wait(whole_dst, part_src, ex):
@@ -157,9 +165,17 @@
     def blk(owner, b):
         return pl.ds(pl.multiple_of(b * seq + owner * tok, tok), tok)
 
-    exchange(lambda p, b: x_hbm.at[p * n_seq + b], lambda p, b: h.at[blk(p, b)], 0)
+    exchange(lambda p, b: x_hbm.at[p * n_seq + b], lambda p, b: h.at[blk(p, b)], 0, range(n_seq))
     for c in in_copies:
         c.start()
+
+    chan[0:CONV, :] = conv_w[...].astype(F32)
+    chan[CONV:CONV + 1, :] = conv_b[...].astype(F32).reshape(1, inner)
+    chan[CONV + 1:CONV + 2, :] = dt_b[...].reshape(1, inner)
+    for j in range(lanes):
+        neg = -jnp.exp(a_log[:, j * 128:(j + 1) * 128]) * LOG2E
+        for m in range(n_state // 8):
+            a2[pl.ds(m * 8 * PITCH + j, 8, stride=PITCH), :] = neg[m * 8:(m + 1) * 8]
 
     def relayout(i, n_heads, unit0, k0):
         slot = lax.rem(i, STAGE)
@@ -167,18 +183,20 @@
         pitch = n_heads + 1
         stage_copy(wq, 0, slot).wait()
 
-        @pl.loop(0, KB * per // 16)
-        def _(g):
-            buf = tmp.at[lax.rem(g, 2)]
-            for r in range(16 // per):
-                val = stage[slot, g * (16 // per) + r].astype(F32)
-                for j in range(per):
-                    buf[pl.ds((r * per + j) * pitch, n_heads), :] = val[j * n_heads:(j + 1) * n_heads]
-            ks = pl.ds(pl.multiple_of(k0 + g * 16, 16), 16)
-            for hd in range(n_heads):
-                w = WN // 128
-                ring[unit0 + hd // w, ks, (hd % w) * 128:(hd % w + 1) * 128] = (
-                    buf[pl.ds(hd, 16, stride=pitch), :].astype(BF16))
+        @pl.loop(0, KB * per // 32)
+        def _(g2):
+            for m in range(2):
+                g = g2 * 2 + m
+                base_row = m * 16 * 33
+                for r in range(16 // per):
+                    val = stage[slot, g * (16 // per) + r].astype(F32)
+                    for j in range(per):
+                        delta[pl.ds(base_row + (r * per + j) * pitch, n_heads), :] = val[j * n_heads:(j + 1) * n_heads]
+                ks = pl.ds(pl.multiple_of(k0 + g * 16, 16), 16)
+                for hd in range(n_heads):
+                    w = WN // 128
+                    ring[unit0 + hd // w, ks, (hd % w) * 128:(hd % w + 1) * 128] = (
+                        delta[pl.ds(base_row + hd, 16, stride=pitch), :].astype(BF16))
 
         stage_start(i + STAGE)
 
@@ -192,12 +210,12 @@
             relayout(n_q + m * n_kv + i, kv_heads, (qdim + m * kv_heads * 128) // WN, i * KB * (32 // kv_heads))
 
     exchange_wait(h, h.at[pl.ds(0, rows - n_seq * tok)], 0)
-    norm_rows(0)
+    norm_rows(attn_g)
 
     def qkv_body(t, w):
         qkv[:, cols(t)] = jnp.dot(a[...], w[...], preferred_element_type=F32).astype(BF16)
 
-    phase(u_qkv, qkv.shape[1] // WN, qkv_body)
+    phase(u_qkv, qkv.shape[1] // WN, qkv_body, 3)
 
     qi = lax.broadcasted_iota(jnp.int32, (seq, seq), 0)
     ki = lax.broadcasted_iota(jnp.int32, (seq, seq), 1)
@@ -224,15 +242,15 @@
         acc += jnp.dot(qkv[:, half_q:qdim], w1[...], preferred_element_type=F32)
         h[:, cols(t)] = (h[:, cols(t)].astype(F32) + acc).astype(BF16)
 
-    phase(u_wo, dim // WN, wo_body)
-    norm_rows(1)
+    phase(u_wo, dim // WN, wo_body, 2)
+    norm_rows(mlp_g)
 
     def gu_body(t, w0, w1):
         g = jnp.dot(a[...], w0[...], preferred_element_type=F32)
         u = jnp.dot(a[...], w1[...], preferred_element_type=F32)
         act[:, cols(t)] = (silu(g) * u).astype(BF16)
 
-    phase(u_gu, ff // WN, gu_body)
+    phase(u_gu, ff // WN, gu_body, 2)
 
     def dn_body(t, *ws):
         acc = None
@@ -242,7 +260,7 @@
         h[:, cols(t)] = (h[:, cols(t)].astype(F32) + acc).astype(BF16)
 
     phase(u_dn, dim // WN, dn_body)
-    norm_rows(2)
+    norm_rows(mamba_g)
 
     row_id = lax.broadcasted_iota(jnp.int32, (seq, 1), 0)
 
@@ -267,14 +285,10 @@
 
     phase(u_wx, inner // WN, wx_body)
 
-    def wz_body(t, w):
-        qkv[:, cols(t)] = jnp.dot(a[...], w[...], preferred_element_type=F32).astype(BF16)
-
-    phase(u_wz, inner // WN, wz_body)
-
     in_copies[0].wait()
     r = lax.dot_general(act[:, :inner], wxp[...], (((1,), (1,)), ((), ())), preferred_element_type=F32)
     n_r = r.shape[1]
+    gain_r = jnp.concatenate([dt_g[...].reshape(1, dt_rank), b_g[...].reshape(1, n_state), c_g[...].reshape(1, n_state)], axis=1)
     col = lax.broadcasted_iota(jnp.int32, (1, n_r), 1)
     sq = r * r
 
@@ -285,18 +299,15 @@
     m_b = (col >= dt_rank) & (col < dt_rank + n_state)
     m_c = col >= dt_rank + n_state
     inv = jnp.where(m_dt, inv_of(m_dt, dt_rank), jnp.where(m_b, inv_of(m_b, n_state), inv_of(m_c, n_state)))
-    rn = r * inv * gains[0:1, :]
-    for n in range(n_state):
-        bb[n * rows:(n + 1) * rows, :] = jnp.broadcast_to(rn[:, dt_rank + n:dt_rank + n + 1], (rows, 128))
-        c0 = dt_rank + n_state + n
-        cb[n * rows:(n + 1) * rows, :] = jnp.broadcast_to(rn[:, c0:c0 + 1], (rows, 128))
+    rn = r * inv * gain_r
+    rn_ref[...] = rn
     dt_in = rn[:, :dt_rank].astype(BF16)
-    a[:, :dt_rank] = dt_in
+    act[:, inner:inner + dt_rank] = dt_in
     in_copies[1].wait()
 
     @pl.loop(0, inner // WN)
     def _(t):
-        pre = jnp.dot(a[:, :dt_rank], wdt[:, cols(t)], preferred_element_type=F32) + chan[5:6, cols(t)]
+        pre = jnp.dot(act[:, inner:inner + dt_rank], wdt[:, cols(t)], preferred_element_type=F32) + chan[5:6, cols(t)]
         step = jnp.maximum(pre, 0.0) + jnp.log1p(jnp.exp(-jnp.abs(pre)))
         for b in range(n_seq):
             scatter(delta, b * seq, t, step[b * seq:(b + 1) * seq])
@@ -304,25 +315,40 @@
     def bcast(ref, idx):
         return jnp.broadcast_to(ref[pl.ds(idx, 1), :], (8, 128))
 
-    @pl.loop(0, n_seq)
-    def _(b):
-        @pl.loop(0, lanes // 8)
-        def _(c):
-            av = [a2[pl.ds(pl.multiple_of(n * lanes + c * 8, 8), 8), :] for n in range(n_state)]
+    toks = 8
+    kc = 512
+    n_zk = dim // kc
+    n_ok = inner // kc
+    n_chunk = lanes // 8
+    z_per = inner // WN // n_chunk
+
+    def send_out(b, t):
+        a[b * seq:(b + 1) * seq, cols(t)] = (
+            h[b * seq:(b + 1) * seq, cols(t)].astype(F32) + acc_ref[b * seq:(b + 1) * seq, :]).astype(BF16)
+        exchange(lambda p, b: a.at[blk(p, b), cols(t)], lambda p, b: out_ref.at[p * n_seq + b, :, cols(t)], 1, [b])
+
+    for b in range(n_seq):
+        for n in range(n_state):
+            for ref, c0 in ((bb, dt_rank + n), (cb, dt_rank + n_state + n)):
+                ref[n * seq:(n + 1) * seq, :] = jnp.broadcast_to(rn_ref[b * seq:(b + 1) * seq, c0:c0 + 1], (seq, 128))
+
+        @pl.loop(0, n_chunk)
+        def _(c, b=b):
+            av = [a2[pl.ds(n * PITCH + c * 8, 8), :] for n in range(n_state)]
             dsk = dskip[pl.ds(pl.multiple_of(c * 8, 8), 8), :]
 
-            def step(i, st):
+            def tokens(i, st):
                 st = list(st)
-                for k in range(4):
-                    r = b * seq + i * 4 + k
-                    at = pl.ds(r * PITCH + c * 8, 8)
+                for k in range(toks):
+                    r = i * toks + k
+                    at = pl.ds((b * seq + r) * PITCH + c * 8, 8)
                     d = delta[at, :]
                     x = xs[at, :]
                     dx = d * x
                     terms = []
                     for n in range(n_state):
-                        st[n] = jnp.exp2(d * av[n]) * st[n] + dx * bcast(bb, n * rows + r)
-                        terms.append(st[n] * bcast(cb, n * rows + r))
+                        st[n] = jnp.exp2(d * av[n]) * st[n] + dx * bcast(bb, n * seq + r)
+                        terms.append(st[n] * bcast(cb, n * seq + r))
                     terms.append(dsk * x)
                     while len(terms) > 1:
                         terms = [terms[m] + terms[m + 1] for m in range(0, len(terms) - 1, 2)] + (
@@ -330,25 +356,56 @@
                     delta[at, :] = terms[0]
                 return tuple(st)
 
-            lax.fori_loop(0, seq // 4, step, tuple(jnp.zeros((8, 128), F32) for _ in range(n_state)))
-
-    @pl.loop(0, rows // 16)
-    def _(i):
-        r0 = pl.multiple_of(i * 16, 16)
-        for j in range(lanes):
-            y = jnp.concatenate([delta[pl.ds((r0 + 8 * m) * PITCH + j, 8, stride=PITCH), :] for m in range(2)], axis=0)
-            z = qkv[pl.ds(r0, 16), j * 128:(j + 1) * 128].astype(F32)
-            act[pl.ds(r0, 16), j * 128:(j + 1) * 128] = (y * silu(z)).astype(BF16)
-
-    def out_body(t, *ws):
+            st = tuple(jnp.zeros((8, 128), F32) for _ in range(n_state))
+            if b == 0:
+                for j in range(z_per):
+                    u = u_wz + c * z_per + j
+                    slot = lax.rem(u, SLOTS)
+                    copy((wz, 0, dim), 0, slot).wait()
+                    acc_ref[...] = jnp.zeros_like(acc_ref)
+
+                    def piece(k, st, slot=slot, j=j):
+                        ks = pl.ds(pl.multiple_of(k * kc, kc), kc)
+                        acc_ref[...] += jnp.dot(a[:, ks], ring[slot, ks, :], preferred_element_type=F32)
+                        return tokens(j * n_zk + k, st)
+
+                    st = lax.fori_loop(0, n_zk, piece, st)
+                    qkv[:, cols(c * z_per + j)] = acc_ref[...].astype(BF16)
+                    start(u + SLOTS, u_wz + SLOTS, u_out + SLOTS)
+                done = z_per * n_zk
+            else:
+                for j in range(2):
+                    copy((wout, 0, unit), 0, lax.rem(u_out + c * 2 + j, SLOTS)).wait()
+                acc_ref[:seq, :] = jnp.zeros((seq, WN), F32)
+
+                def piece(k, st):
+                    half = n_ok // 2
+                    slot = lax.rem(u_out + c * 2 + lax.div(k, half), SLOTS)
+                    ks = pl.ds(pl.multiple_of(k * kc, kc), kc)
+                    kw = pl.ds(pl.multiple_of(lax.rem(k, half) * kc, kc), kc)
+                    acc_ref[:seq, :] += jnp.dot(act[:seq, ks], ring[slot, kw, :], preferred_element_type=F32)
+                    return tokens(k, st)
+
+                st = lax.fori_loop(0, n_ok, piece, st)
+                send_out(0, c)
+                done = n_ok
+            lax.fori_loop(done, seq // toks, tokens, st)
+
+        @pl.loop(0, seq // 16)
+        def _(i, b=b):
+            r0 = pl.multiple_of(b * seq + i * 16, 16)
+            for j in range(lanes):
+                y = jnp.concatenate([delta[pl.ds((r0 + 8 * m) * PITCH + j, 8, stride=PITCH), :] for m in range(2)], axis=0)
+                z = qkv[pl.ds(r0, 16), j * 128:(j + 1) * 128].astype(F32)
+                act[pl.ds(r0, 16), j * 128:(j + 1) * 128] = (y * silu(z)).astype(BF16)
+
+    for t in range(dim // WN):
         acc = None
-        for (s, n), w in zip(chunks(inner), ws):
-            d = jnp.dot(act[:, s:s + n], w[...], preferred_element_type=F32)
+        for j, (s, n) in enumerate(chunks(inner)):
+            d = jnp.dot(act[seq:, s:s + n], ring[(u_out + 2 * t + j) % SLOTS, :n], preferred_element_type=F32)
             acc = d if acc is None else acc + d
-        a[:, cols(t)] = (h[:, cols(t)].astype(F32) + acc).astype(BF16)
-        exchange(lambda p, b: a.at[blk(p, b), cols(t)], lambda p, b: out_ref.at[p * n_seq + b, :, cols(t)], 1)
-
-    phase(u_out, dim // WN, out_body)
+        acc_ref[seq:, :] = acc
+        send_out(1, t)
     exchange_wait(out_ref, a.at[pl.ds(0, rows - n_seq * tok)], 1)
 
 
@@ -357,34 +414,31 @@
     n_seq = n_batch // lax.axis_size("sp")
     rows = n_batch * tok
     inner, n_state = a_log.shape
-    lanes = inner // 128
-    norms = jnp.stack([attn_norm, mlp_norm, mamba_norm]).astype(F32)
-    chan = jnp.concatenate([conv_w.astype(F32), conv_b.astype(F32)[None], dt_bias[None], jnp.zeros((2, inner), F32)])
-    gains = jnp.concatenate([dt_norm, b_norm, c_norm])[None]
-    a2 = (-jnp.exp(a_log.T) * LOG2E).reshape(n_state * lanes, 128)
-    dskip = d_skip.reshape(lanes, 128)
     hbm = pl.BlockSpec(memory_space=pltpu.HBM)
     vm = pl.BlockSpec(memory_space=pltpu.VMEM)
     qkv_dim = (w_q.shape[1] + w_k.shape[1] + w_v.shape[1]) * 128
     return pl.pallas_call(
         block_kernel,
         out_shape=jax.ShapeDtypeStruct(hidden.shape, BF16),
-        in_specs=[hbm] * 13 + [vm] * 5,
+        in_specs=[hbm] * 13 + [vm] * 11,
         out_specs=hbm,
         scratch_shapes=[
             pltpu.VMEM((SLOTS, dim, WN), BF16),
             pltpu.VMEM((STAGE, KB, 32, 128), BF16),
-            pltpu.VMEM((2, 16 * 33, 128), F32),
+            pltpu.VMEM((rows, WN), F32),
             pltpu.VMEM((rows, qkv_dim), BF16),
             pltpu.VMEM((rows, dim), BF16),
             pltpu.VMEM((rows, dim), BF16),
             pltpu.VMEM((rows, w_gate.shape[1]), BF16),
             pltpu.VMEM((rows * PITCH, 128), F32),
             pltpu.VMEM((rows * PITCH, 128), F32),
-            pltpu.VMEM((rows * n_state, 128), F32),
-            pltpu.VMEM((rows * n_state, 128), F32),
+            pltpu.VMEM((128 * n_state, 128), F32),
+            pltpu.VMEM((128 * n_state, 128), F32),
             pltpu.VMEM((w_xproj.shape[1], inner), BF16),
             pltpu.VMEM(w_dt.shape, BF16),
+            pltpu.VMEM((n_state * PITCH, 128), F32),
+            pltpu.VMEM((8, inner), F32),
+            pltpu.VMEM((rows, w_xproj.shape[1]), F32),
             pltpu.SemaphoreType.DMA((SLOTS,)),
             pltpu.SemaphoreType.DMA((STAGE,)),
             pltpu.SemaphoreType.DMA((2,)),
@@ -394,7 +448,8 @@
         compiler_params=pltpu.CompilerParams(vmem_limit_bytes=67043328, collective_id=0, has_side_effects=True),
         name="block",
     )(hidden, w_q.reshape(-1, 32, 128), w_k.reshape(-1, 32, 128), w_v.reshape(-1, 32, 128), w_o.reshape(-1, dim),
-      w_gate, w_up, w_down, w_in_x, w_in_z, w_xproj.T, w_dt, w_out, norms, chan, gains, dskip, a2)
+      w_gate, w_up, w_down, w_in_x, w_in_z, w_xproj.T, w_dt, w_out, attn_norm, mlp_norm, mamba_norm, conv_w, conv_b,
+      dt_norm, b_norm, c_norm, dt_bias, d_skip.reshape(-1, 128), a_log.T)
 
 
 def solution(mesh):

time: 179 us -> 169 us (0.944)
  other arithmetic: 6 us -> 0 us
  local copies, waits for them, and re-layouts: 5.41 us -> 2.46 us
    concatenate x2 -> x0, other arithmetic: 2.82 us -> none  [the longest x1 1.47 us: layer_pair(): jnp.concatenate([conv_w.astype(F32), conv_b.astype(F32)[None], dt_bias[No...]
    another operation x3 -> x0, local copies, waits for them, and re-layouts: 2.1 us -> none  [layer_pair(): norms = jnp.stack([attn_norm, mlp_norm, mamba_norm]).astype(F32)]
where the time goes in v3:
time: 169 us
  Pallas kernels  166 us (98%)
  local copies, waits for them, and re-layouts  2.46 us (1%)
    pallas_call x1, Pallas kernels, layer_pair(): pl.pallas_call(block_kernel, out_shape=jax.ShapeDtypeStruct(hidden.shape,...  166 us

profile of v3, /device:TPU:0, one launch (start us, length us, event | category | flops | bytes accessed | tf_op | source)
XLA Modules:
  0.0 168.8 jit_solution(15763863915367831289)
XLA Ops:
  0.0 166.3 %block.1 = bf16[16,16,2560]{2,1,0:T(8,128)(2,1)} custom-call(bf16[16,16,2560]{2,1,0:T(8,128)(2,1)} %x_hbm.1, bf16[2560,32,128]{2,1,0:T(8,128)(2,1)} %wq.1, bf16[640,32,128]{2,1,0:T(8,128)(2,1)} %bitcast.7, bf16[640,32,128]{2,1,0:T(8,128)(2,1)} %bitcast.8, bf16[4096,2560]{1,0:T(8,128)(2,1)} %bitcast.6, bf16[2560,9728]{1,0:T(8,128)(2,1)} %wg.1, ...), custom_call_target="tpu_custom_call" | custom-call | tf_op jit(solution)/shard_map/block/pallas_call | solution.py:420
  166.3 2.5 %copy.26 = bf16[16,16,2560]{2,1,0:T(8,128)(2,1)} copy(bf16[16,16,2560]{2,1,0:T(8,128)(2,1)} %block.1) | data formatting | bytes 2621440

commit v4 on v3

--- a/solution.py
+++ b/solution.py
@@ -32,7 +32,7 @@
 
 def block_kernel(x_hbm, wq, wk, wv, wo, wg, wu, wd, wx, wz, wxp_hbm, wdt_hbm, wout,
                  attn_g, mlp_g, mamba_g, conv_w, conv_b, dt_g, b_g, c_g, dt_b, dskip, a_log, out_ref,
-                 ring, stage, acc_ref, qkv, h, a, act, delta, xs, bb, cb, wxp, wdt, a2, chan, rn_ref,
+                 ring, stage, qkv, h, a, act, delta, xs, bb, cb, wxp, wdt, a2, chan, rn_ref,
                  ring_sem, stage_sem, in_sem, send_sem, recv_sem):
     rows, dim = h.shape
     n_seq, seq = 2, 128
@@ -283,7 +283,7 @@
             act[b * seq:(b + 1) * seq, cols(t)] = c
             scatter(xs, b * seq, t, c.astype(F32))
 
-    phase(u_wx, inner // WN, wx_body)
+    phase(u_wx, inner // WN, wx_body, 2)
 
     in_copies[0].wait()
     r = lax.dot_general(act[:, :inner], wxp[...], (((1,), (1,)), ((), ())), preferred_element_type=F32)
@@ -305,34 +305,27 @@
     act[:, inner:inner + dt_rank] = dt_in
     in_copies[1].wait()
 
-    @pl.loop(0, inner // WN)
-    def _(t):
-        pre = jnp.dot(act[:, inner:inner + dt_rank], wdt[:, cols(t)], preferred_element_type=F32) + chan[5:6, cols(t)]
+    def wz_body(t, w):
+        pre = jnp.dot(act[:, inner:inner + dt_rank], wdt[:, cols(t)], preferred_element_type=F32)
+        qkv[:, cols(t)] = jnp.dot(a[...], w[...], preferred_element_type=F32).astype(BF16)
+        pre = pre + chan[5:6, cols(t)]
         step = jnp.maximum(pre, 0.0) + jnp.log1p(jnp.exp(-jnp.abs(pre)))
         for b in range(n_seq):
             scatter(delta, b * seq, t, step[b * seq:(b + 1) * seq])
 
+    phase(u_wz, inner // WN, wz_body, 2)
+
     def bcast(ref, idx):
         return jnp.broadcast_to(ref[pl.ds(idx, 1), :], (8, 128))
 
     toks = 8
-    kc = 512
-    n_zk = dim // kc
-    n_ok = inner // kc
-    n_chunk = lanes // 8
-    z_per = inner // WN // n_chunk
-
-    def send_out(b, t):
-        a[b * seq:(b + 1) * seq, cols(t)] = (
-            h[b * seq:(b + 1) * seq, cols(t)].astype(F32) + acc_ref[b * seq:(b + 1) * seq, :]).astype(BF16)
-        exchange(lambda p, b: a.at[blk(p, b), cols(t)], lambda p, b: out_ref.at[p * n_seq + b, :, cols(t)], 1, [b])
 
     for b in range(n_seq):
         for n in range(n_state):
             for ref, c0 in ((bb, dt_rank + n), (cb, dt_rank + n_state + n)):
                 ref[n * seq:(n + 1) * seq, :] = jnp.broadcast_to(rn_ref[b * seq:(b + 1) * seq, c0:c0 + 1], (seq, 128))
 
-        @pl.loop(0, n_chunk)
+        @pl.loop(0, lanes // 8)
         def _(c, b=b):
             av = [a2[pl.ds(n * PITCH + c * 8, 8), :] for n in range(n_state)]
             dsk = dskip[pl.ds(pl.multiple_of(c * 8, 8), 8), :]
@@ -357,39 +350,7 @@
                 return tuple(st)
 
             st = tuple(jnp.zeros((8, 128), F32) for _ in range(n_state))
-            if b == 0:
-                for j in range(z_per):
-                    u = u_wz + c * z_per + j
-                    slot = lax.rem(u, SLOTS)
-                    copy((wz, 0, dim), 0, slot).wait()
-                    acc_ref[...] = jnp.zeros_like(acc_ref)
-
-                    def piece(k, st, slot=slot, j=j):
-                        ks = pl.ds(pl.multiple_of(k * kc, kc), kc)
-                        acc_ref[...] += jnp.dot(a[:, ks], ring[slot, ks, :], preferred_element_type=F32)
-                        return tokens(j * n_zk + k, st)
-
-                    st = lax.fori_loop(0, n_zk, piece, st)
-                    qkv[:, cols(c * z_per + j)] = acc_ref[...].astype(BF16)
-                    start(u + SLOTS, u_wz + SLOTS, u_out + SLOTS)
-                done = z_per * n_zk
-            else:
-                for j in range(2):
-                    copy((wout, 0, unit), 0, lax.rem(u_out + c * 2 + j, SLOTS)).wait()
-                acc_ref[:seq, :] = jnp.zeros((seq, WN), F32)
-
-                def piece(k, st):
-                    half = n_ok // 2
-                    slot = lax.rem(u_out + c * 2 + lax.div(k, half), SLOTS)
-                    ks = pl.ds(pl.multiple_of(k * kc, kc), kc)
-                    kw = pl.ds(pl.multiple_of(lax.rem(k, half) * kc, kc), kc)
-                    acc_ref[:seq, :] += jnp.dot(act[:seq, ks], ring[slot, kw, :], preferred_element_type=F32)
-                    return tokens(k, st)
-
-                st = lax.fori_loop(0, n_ok, piece, st)
-                send_out(0, c)
-                done = n_ok
-            lax.fori_loop(done, seq // toks, tokens, st)
+            lax.fori_loop(0, seq // toks, tokens, st)
 
         @pl.loop(0, seq // 16)
         def _(i, b=b):
@@ -399,13 +360,18 @@
                 z = qkv[pl.ds(r0, 16), j * 128:(j + 1) * 128].astype(F32)
                 act[pl.ds(r0, 16), j * 128:(j + 1) * 128] = (y * silu(z)).astype(BF16)
 
-    for t in range(dim // WN):
-        acc = None
-        for j, (s, n) in enumerate(chunks(inner)):
-            d = jnp.dot(act[seq:, s:s + n], ring[(u_out + 2 * t + j) % SLOTS, :n], preferred_element_type=F32)
-            acc = d if acc is None else acc + d
-        acc_ref[seq:, :] = acc
-        send_out(1, t)
+        rs = pl.ds(b * seq, seq)
+        @pl.loop(0, dim // WN)
+        def _(t, b=b, rs=rs):
+            views = []
+            for j, (s, n) in enumerate(chunks(inner)):
+                slot = lax.rem(u_out + 2 * t + j, SLOTS)
+                if b == 0:
+                    copy((wout, s, n), 0, slot).wait()
+                views.append(jnp.dot(act[rs, s:s + n], ring[slot, :n], preferred_element_type=F32))
+            a[rs, cols(t)] = (h[rs, cols(t)].astype(F32) + (views[0] + views[1])).astype(BF16)
+            exchange(lambda p, b: a.at[blk(p, b), cols(t)], lambda p, b: out_ref.at[p * n_seq + b, :, cols(t)], 1, [b])
+
     exchange_wait(out_ref, a.at[pl.ds(0, rows - n_seq * tok)], 1)
 
 
@@ -425,7 +391,6 @@
         scratch_shapes=[
             pltpu.VMEM((SLOTS, dim, WN), BF16),
             pltpu.VMEM((STAGE, KB, 32, 128), BF16),
-            pltpu.VMEM((rows, WN), F32),
             pltpu.VMEM((rows, qkv_dim), BF16),
             pltpu.VMEM((rows, dim), BF16),
             pltpu.VMEM((rows, dim), BF16),

time: 169 us -> 154 us (0.911)
  Pallas kernels: 166 us -> 152 us
    pallas_call x1, Pallas kernels: 166 us -> 152 us  [layer_pair(): pl.pallas_call(block_kernel, out_shape=jax.ShapeDtypeStruct(hidden.shape,...]
where the time goes in v4:
time: 154 us
  Pallas kernels  152 us (99%)
  local copies, waits for them, and re-layouts  2.46 us (2%)
    pallas_call x1, Pallas kernels, layer_pair(): pl.pallas_call(block_kernel, out_shape=jax.ShapeDtypeStruct(hidden.shape,...  152 us

profile of v4, /device:TPU:0, one launch (start us, length us, event | category | flops | bytes accessed | tf_op | source)
XLA Modules:
  0.0 154.1 jit_solution(17796431116575880996)
XLA Ops:
  0.0 151.6 %block.1 = bf16[16,16,2560]{2,1,0:T(8,128)(2,1)} custom-call(bf16[16,16,2560]{2,1,0:T(8,128)(2,1)} %x_hbm.1, bf16[2560,32,128]{2,1,0:T(8,128)(2,1)} %wq.1, bf16[640,32,128]{2,1,0:T(8,128)(2,1)} %bitcast.7, bf16[640,32,128]{2,1,0:T(8,128)(2,1)} %bitcast.8, bf16[4096,2560]{1,0:T(8,128)(2,1)} %bitcast.6, bf16[2560,9728]{1,0:T(8,128)(2,1)} %wg.1, ...), custom_call_target="tpu_custom_call" | custom-call | tf_op jit(solution)/shard_map/block/pallas_call | solution.py:386
  151.6 2.5 %copy.26 = bf16[16,16,2560]{2,1,0:T(8,128)(2,1)} copy(bf16[16,16,2560]{2,1,0:T(8,128)(2,1)} %block.1) | data formatting | bytes 2621440

commit v5 on v4

--- a/solution.py
+++ b/solution.py
@@ -212,30 +212,51 @@
     exchange_wait(h, h.at[pl.ds(0, rows - n_seq * tok)], 0)
     norm_rows(attn_g)
 
-    def qkv_body(t, w):
-        qkv[:, cols(t)] = jnp.dot(a[...], w[...], preferred_element_type=F32).astype(BF16)
-
-    phase(u_qkv, qkv.shape[1] // WN, qkv_body, 3)
+    def project(u):
+        return jnp.dot(a[...], ring[u], preferred_element_type=F32).astype(BF16)
+
+    n_qu = qdim // WN
+    n_qkv = qkv.shape[1] // WN
+    for u in list(range(n_qu, n_qkv)) + [0, 1]:
+        qkv[:, u * WN:(u + 1) * WN] = project(u)
+    for u in list(range(n_qu, n_qkv)) + [0, 1]:
+        start(jnp.int32(u + SLOTS), u + SLOTS, u + SLOTS)
 
     qi = lax.broadcasted_iota(jnp.int32, (seq, seq), 0)
     ki = lax.broadcasted_iota(jnp.int32, (seq, seq), 1)
     causal = jnp.concatenate([qi >= ki] * groups, axis=0)
 
-    @pl.loop(0, kv_heads)
-    def _(kvh):
-        for b in range(n_seq):
-            rs = pl.ds(b * seq, seq)
+    def attend(kvh, unit):
+        qcols = [pl.ds(pl.multiple_of((kvh * groups + i) * 128, 128), 128) for i in range(groups)]
+        rss = [pl.ds(b * seq, seq) for b in range(n_seq)]
+        scores = []
+        for rs in rss:
             kk = qkv[rs, pl.ds(pl.multiple_of(qdim + kvh * 128, 128), 128)]
+            qq = jnp.concatenate([qkv[rs, c] for c in qcols], axis=0)
+            scores.append(lax.dot_general(qq, kk, (((1,), (1,)), ((), ())), preferred_element_type=F32))
+        nxt = None if unit is None else project(unit)
+        probs = []
+        for s in scores:
+            s = jnp.where(causal, s * 128 ** -0.5, -jnp.inf)
+            e = jnp.exp(s - jnp.max(s, axis=-1, keepdims=True))
+            probs.append((e * (1.0 / jnp.sum(e, axis=-1, keepdims=True))).astype(BF16))
+        for rs, p in zip(rss, probs):
             vv = qkv[rs, pl.ds(pl.multiple_of(qdim + (kv_heads + kvh) * 128, 128), 128)]
-            qcols = [pl.ds(pl.multiple_of((kvh * groups + i) * 128, 128), 128) for i in range(groups)]
-            qq = jnp.concatenate([qkv[rs, c] for c in qcols], axis=0)
-            s = lax.dot_general(qq, kk, (((1,), (1,)), ((), ())), preferred_element_type=F32) * 128 ** -0.5
-            s = jnp.where(causal, s, -jnp.inf)
-            e = jnp.exp(s - jnp.max(s, axis=-1, keepdims=True))
-            p = (e * (1.0 / jnp.sum(e, axis=-1, keepdims=True))).astype(BF16)
             o = jnp.dot(p, vv, preferred_element_type=F32).astype(BF16)
             for i, c in enumerate(qcols):
                 qkv[rs, c] = o[i * seq:(i + 1) * seq]
+        return nxt
+
+    @pl.loop(0, kv_heads // 2 - 1)
+    def _(i):
+        nxt = [attend(2 * i + m, 2 * i + 2 + m) for m in range(2)]
+        for m in range(2):
+            qkv[:, cols(2 * i + 2 + m)] = nxt[m]
+        for m in range(2):
+            start(2 * i + 2 + m + SLOTS, SLOTS + 2, SLOTS + n_qu - 1)
+
+    for m in range(2):
+        attend(jnp.int32(kv_heads - 2 + m), None)
 
     def wo_body(t, w0, w1):
         acc = jnp.dot(qkv[:, :half_q], w0[...], preferred_element_type=F32)

time: 154 us -> 149 us (0.968)
  Pallas kernels: 152 us -> 146 us
    pallas_call x1, Pallas kernels: 152 us -> 146 us  [layer_pair(): pl.pallas_call(block_kernel, out_shape=jax.ShapeDtypeStruct(hidden.shape,...]
where the time goes in v5:
time: 149 us
  Pallas kernels  146 us (98%)
  local copies, waits for them, and re-layouts  2.46 us (2%)
    pallas_call x1, Pallas kernels, layer_pair(): pl.pallas_call(block_kernel, out_shape=jax.ShapeDtypeStruct(hidden.shape,...  146 us

profile of v5, /device:TPU:0, one launch (start us, length us, event | category | flops | bytes accessed | tf_op | source)
XLA Modules:
  0.0 148.8 jit_solution(10287384883623339782)
XLA Ops:
  0.0 146.4 %block.1 = bf16[16,16,2560]{2,1,0:T(8,128)(2,1)} custom-call(bf16[16,16,2560]{2,1,0:T(8,128)(2,1)} %x_hbm.1, bf16[2560,32,128]{2,1,0:T(8,128)(2,1)} %wq.1, bf16[640,32,128]{2,1,0:T(8,128)(2,1)} %bitcast.7, bf16[640,32,128]{2,1,0:T(8,128)(2,1)} %bitcast.8, bf16[4096,2560]{1,0:T(8,128)(2,1)} %bitcast.6, bf16[2560,9728]{1,0:T(8,128)(2,1)} %wg.1, ...), custom_call_target="tpu_custom_call" | custom-call | tf_op jit(solution)/shard_map/block/pallas_call | solution.py:407
  146.4 2.5 %copy.26 = bf16[16,16,2560]{2,1,0:T(8,128)(2,1)} copy(bf16[16,16,2560]{2,1,0:T(8,128)(2,1)} %block.1) | data formatting | bytes 2621440

commit v6 on v5

--- a/solution.py
+++ b/solution.py
@@ -116,12 +116,13 @@
     def norm_rows(g_ref):
         gain = g_ref[...].astype(F32).reshape(1, dim)
 
-        @pl.loop(0, rows // 32)
+        @pl.loop(0, rows // 64)
         def _(i):
-            rs = pl.ds(pl.multiple_of(i * 32, 32), 32)
-            hv = h[rs, :].astype(F32)
-            inv = lax.rsqrt(jnp.mean(hv * hv, axis=-1, keepdims=True) + EPS)
-            a[rs, :] = (hv * inv * gain).astype(BF16)
+            for m in range(4):
+                rs = pl.ds(pl.multiple_of(i * 64 + m * 16, 16), 16)
+                hv = h[rs, :].astype(F32)
+                inv = lax.rsqrt(jnp.mean(hv * hv, axis=-1, keepdims=True) + EPS)
+                a[rs, :] = (h[rs, :].astype(F32) * inv * gain).astype(BF16)
 
     in_copies = [
         pltpu.make_async_copy(wxp_hbm, wxp, in_sem.at[0]),
@@ -384,13 +385,13 @@
         rs = pl.ds(b * seq, seq)
         @pl.loop(0, dim // WN)
         def _(t, b=b, rs=rs):
-            views = []
-            for j, (s, n) in enumerate(chunks(inner)):
-                slot = lax.rem(u_out + 2 * t + j, SLOTS)
-                if b == 0:
+            slots = [lax.rem(u_out + 2 * t + j, SLOTS) for j in range(2)]
+            if b == 0:
+                for (s, n), slot in zip(chunks(inner), slots):
                     copy((wout, s, n), 0, slot).wait()
-                views.append(jnp.dot(act[rs, s:s + n], ring[slot, :n], preferred_element_type=F32))
-            a[rs, cols(t)] = (h[rs, cols(t)].astype(F32) + (views[0] + views[1])).astype(BF16)
+            ds = [jnp.dot(act[rs, s:s + n], ring[slot, :n], preferred_element_type=F32)
+                  for (s, n), slot in zip(chunks(inner), slots)]
+            a[rs, cols(t)] = (h[rs, cols(t)].astype(F32) + (ds[0] + ds[1])).astype(BF16)
             exchange(lambda p, b: a.at[blk(p, b), cols(t)], lambda p, b: out_ref.at[p * n_seq + b, :, cols(t)], 1, [b])
 
     exchange_wait(out_ref, a.at[pl.ds(0, rows - n_seq * tok)], 1)

time: 149 us -> 147 us (0.987)
  Pallas kernels: 146 us -> 144 us
    pallas_call x1, Pallas kernels: 146 us -> 144 us  [layer_pair(): pl.pallas_call(block_kernel, out_shape=jax.ShapeDtypeStruct(hidden.shape,...]
where the time goes in v6:
time: 147 us
  Pallas kernels  144 us (98%)
  local copies, waits for them, and re-layouts  2.46 us (2%)
    pallas_call x1, Pallas kernels, layer_pair(): pl.pallas_call(block_kernel, out_shape=jax.ShapeDtypeStruct(hidden.shape,...  144 us

profile of v6, /device:TPU:0, one launch (start us, length us, event | category | flops | bytes accessed | tf_op | source)
XLA Modules:
  0.0 146.6 jit_solution(3015777005474398654)
XLA Ops:
  0.0 144.1 %block.1 = bf16[16,16,2560]{2,1,0:T(8,128)(2,1)} custom-call(bf16[16,16,2560]{2,1,0:T(8,128)(2,1)} %x_hbm.1, bf16[2560,32,128]{2,1,0:T(8,128)(2,1)} %wq.1, bf16[640,32,128]{2,1,0:T(8,128)(2,1)} %bitcast.7, bf16[640,32,128]{2,1,0:T(8,128)(2,1)} %bitcast.8, bf16[4096,2560]{1,0:T(8,128)(2,1)} %bitcast.6, bf16[2560,9728]{1,0:T(8,128)(2,1)} %wg.1, ...), custom_call_target="tpu_custom_call" | custom-call | tf_op jit(solution)/shard_map/block/pallas_call | solution.py:408
  144.2 2.5 %copy.26 = bf16[16,16,2560]{2,1,0:T(8,128)(2,1)} copy(bf16[16,16,2560]{2,1,0:T(8,128)(2,1)} %block.1) | data formatting | bytes 2621440

commit v7 on v6

--- a/solution.py
+++ b/solution.py
@@ -102,7 +102,7 @@
                     copy(part, 0, slot).wait()
                 views.append(ring.at[slot, pl.ds(0, part[2])])
             for m in range(count):
-                body(t0 + m, *views[m * n:(m + 1) * n])
+                body(t0 + m, *views[m * n:(m + 1) * n], **({'parity': m % 2} if body.__name__ == 'wx_body' else {}))
             for u in range(count * n):
                 start(first + t0 * n + u + SLOTS, first + SLOTS, first + SLOTS + n_tiles * n - 1)
 
@@ -292,18 +292,27 @@
                 dst[pl.ds((r0 + i * 8) * PITCH + t * (WN // 128) + j, 8, stride=PITCH), :] = (
                     val[i * 8:(i + 1) * 8, j * 128:(j + 1) * 128])
 
-    def wx_body(t, w):
+    conv_pitch = seq + 8
+    for k in range(2 * n_seq * (WN // 128)):
+        delta[k * conv_pitch:k * conv_pitch + 8, :] = jnp.zeros((8, 128), F32)
+
+    def wx_body(t, w, parity=0):
         res = jnp.dot(a[...], w[...], preferred_element_type=F32).astype(BF16).astype(F32)
         for b in range(n_seq):
-            xi = res[b * seq:(b + 1) * seq]
-            acc = chan[4:5, cols(t)] + chan[CONV - 1:CONV, cols(t)] * xi
-            for j in range(CONV - 1):
-                back = CONV - 1 - j
-                prev = jnp.where(row_id >= back, pltpu.roll(xi, back, axis=0), 0.0)
-                acc += chan[j:j + 1, cols(t)] * prev
-            c = silu(acc).astype(BF16)
-            act[b * seq:(b + 1) * seq, cols(t)] = c
-            scatter(xs, b * seq, t, c.astype(F32))
+            for j in range(WN // 128):
+                top = ((parity * n_seq + b) * (WN // 128) + j) * conv_pitch + 8
+                cj = pl.ds(pl.multiple_of(t * WN, WN) + j * 128, 128)
+                xi = res[b * seq:(b + 1) * seq, j * 128:(j + 1) * 128]
+                delta[top:top + seq, :] = xi
+                acc = chan[4:5, cj] + chan[CONV - 1:CONV, cj] * xi
+                for k in range(CONV - 1):
+                    back = CONV - 1 - k
+                    acc += chan[k:k + 1, cj] * delta[top - back:top - back + seq, :]
+                c = silu(acc).astype(BF16)
+                act[b * seq:(b + 1) * seq, cj] = c
+                cf = c.astype(F32)
+                for i in range(seq // 8):
+                    xs[pl.ds((b * seq + i * 8) * PITCH + t * (WN // 128) + j, 8, stride=PITCH), :] = cf[i * 8:(i + 1) * 8]
 
     phase(u_wx, inner // WN, wx_body, 2)
 
@@ -383,16 +392,17 @@
                 act[pl.ds(r0, 16), j * 128:(j + 1) * 128] = (y * silu(z)).astype(BF16)
 
         rs = pl.ds(b * seq, seq)
-        @pl.loop(0, dim // WN)
-        def _(t, b=b, rs=rs):
-            slots = [lax.rem(u_out + 2 * t + j, SLOTS) for j in range(2)]
-            if b == 0:
-                for (s, n), slot in zip(chunks(inner), slots):
-                    copy((wout, s, n), 0, slot).wait()
-            ds = [jnp.dot(act[rs, s:s + n], ring[slot, :n], preferred_element_type=F32)
-                  for (s, n), slot in zip(chunks(inner), slots)]
-            a[rs, cols(t)] = (h[rs, cols(t)].astype(F32) + (ds[0] + ds[1])).astype(BF16)
-            exchange(lambda p, b: a.at[blk(p, b), cols(t)], lambda p, b: out_ref.at[p * n_seq + b, :, cols(t)], 1, [b])
+        n_t = dim // WN
+        if b == 0:
+            for t in range(n_t):
+                for j, (s, n) in enumerate(chunks(inner)):
+                    copy((wout, s, n), 0, (u_out + 2 * t + j) % SLOTS).wait()
+        for t in range(n_t):
+            ct = pl.ds(t * WN, WN)
+            ds = [jnp.dot(act[rs, s:s + n], ring[(u_out + 2 * t + j) % SLOTS, :n], preferred_element_type=F32)
+                  for j, (s, n) in enumerate(chunks(inner))]
+            a[rs, ct] = (h[rs, ct].astype(F32) + (ds[0] + ds[1])).astype(BF16)
+            exchange(lambda p, b: a.at[blk(p, b), ct], lambda p, b: out_ref.at[p * n_seq + b, :, ct], 1, [b])
 
     exchange_wait(out_ref, a.at[pl.ds(0, rows - n_seq * tok)], 1)
 

time: 147 us -> 147 us (level)
  no operation moved by 1% of the time
where the time goes in v7:
time: 147 us; the launch traced here: 146 us
  Pallas kernels  144 us (98%)
  local copies, waits for them, and re-layouts  2.46 us (2%)
    pallas_call x1, Pallas kernels, layer_pair(): pl.pallas_call(block_kernel, out_shape=jax.ShapeDtypeStruct(hidden.shape,...  144 us

profile of v7, /device:TPU:0, one launch (start us, length us, event | category | flops | bytes accessed | tf_op | source)
XLA Modules:
  0.0 146.3 jit_solution(14832511827753510214)
XLA Ops:
  0.0 143.8 %block.1 = bf16[16,16,2560]{2,1,0:T(8,128)(2,1)} custom-call(bf16[16,16,2560]{2,1,0:T(8,128)(2,1)} %x_hbm.1, bf16[2560,32,128]{2,1,0:T(8,128)(2,1)} %wq.1, bf16[640,32,128]{2,1,0:T(8,128)(2,1)} %bitcast.7, bf16[640,32,128]{2,1,0:T(8,128)(2,1)} %bitcast.8, bf16[4096,2560]{1,0:T(8,128)(2,1)} %bitcast.6, bf16[2560,9728]{1,0:T(8,128)(2,1)} %wg.1, ...), custom_call_target="tpu_custom_call" | custom-call | tf_op jit(solution)/shard_map/block/pallas_call | solution.py:418
  143.8 2.5 %copy.26 = bf16[16,16,2560]{2,1,0:T(8,128)(2,1)} copy(bf16[16,16,2560]{2,1,0:T(8,128)(2,1)} %block.1) | data formatting | bytes 2621440

commit v8 on v7

--- a/solution.py
+++ b/solution.py
@@ -349,7 +349,7 @@
     def bcast(ref, idx):
         return jnp.broadcast_to(ref[pl.ds(idx, 1), :], (8, 128))
 
-    toks = 8
+    toks = 16
 
     for b in range(n_seq):
         for n in range(n_state):

time: 147 us -> 146 us (level)
  no operation moved by 1% of the time
where the time goes in v8:
time: 146 us; the launch traced here: 145 us
  Pallas kernels  143 us (98%)
  local copies, waits for them, and re-layouts  2.46 us (2%)
    pallas_call x1, Pallas kernels, layer_pair(): pl.pallas_call(block_kernel, out_shape=jax.ShapeDtypeStruct(hidden.shape,...  143 us

profile of v8, /device:TPU:0, one launch (start us, length us, event | category | flops | bytes accessed | tf_op | source)
XLA Modules:
  0.0 145.3 jit_solution(6515041910019797723)
XLA Ops:
  0.0 142.8 %block.1 = bf16[16,16,2560]{2,1,0:T(8,128)(2,1)} custom-call(bf16[16,16,2560]{2,1,0:T(8,128)(2,1)} %x_hbm.1, bf16[2560,32,128]{2,1,0:T(8,128)(2,1)} %wq.1, bf16[640,32,128]{2,1,0:T(8,128)(2,1)} %bitcast.7, bf16[640,32,128]{2,1,0:T(8,128)(2,1)} %bitcast.8, bf16[4096,2560]{1,0:T(8,128)(2,1)} %bitcast.6, bf16[2560,9728]{1,0:T(8,128)(2,1)} %wg.1, ...), custom_call_target="tpu_custom_call" | custom-call | tf_op jit(solution)/shard_map/block/pallas_call | solution.py:418
  142.9 2.5 %copy.26 = bf16[16,16,2560]{2,1,0:T(8,128)(2,1)} copy(bf16[16,16,2560]{2,1,0:T(8,128)(2,1)} %block.1) | data formatting | bytes 2621440
